TPU v7x, 8 devices: a whole 2x2x1 slice. The times are simulated.
8 devices in a mesh: tube: 2 (over z, y), col: 2 (over x), row: 2 (over core).
Axes of the slice: x: 2, y: 2, z: 1, core: 2. Of those that a mesh axis runs over, the one named last changes fastest.
Arguments:
- tensor: float32 [32, 512, 2048], P('tube', 'row', 'col')
- b_init: float32 [2048, 64], P(('col', 'row', 'tube'))
- c_init: float32 [32, 64], replicated
- ridge_lam: float32 [], replicated
Outputs:
- output 1: float32 [512, 64], P(('row', 'col', 'tube'))
- output 2: float32 [2048, 64], P(('col', 'row', 'tube'))
- output 3: float32 [32, 64], replicated
All inputs are finite; a program needn't handle non-finite values.
Results may differ from a plain program's by a relative error of at most 0.001.
Values are sent between devices in bfloat16 or wider.
A program may use at most 1 GiB of HBM per device.

v0:
```python
import jax
import jax.numpy as jnp
from jax import lax
from jax.sharding import PartitionSpec as P, NamedSharding

SWEEPS = 2
ALL_AXES = ("tube", "col", "row")


def gram_of(factor):
    half_fac = factor.astype(jnp.bfloat16)
    return lax.dot_general(half_fac, half_fac, (((0,), (0,)), ((), ())), preferred_element_type=jnp.float32)


def solve_rows(mttkrp_rows, gram_prod, ridge_lam):
    ident_mat = jnp.eye(gram_prod.shape[0], dtype=jnp.float32)
    chol_fac = jnp.linalg.cholesky(gram_prod + ridge_lam * ident_mat)
    half_solve = lax.linalg.triangular_solve(chol_fac, mttkrp_rows, left_side=False, lower=True, transpose_a=True)
    return lax.linalg.triangular_solve(chol_fac, half_solve, left_side=False, lower=True)


def solution(mesh):
    full_prec = lax.Precision.HIGHEST

    def local_sweeps(x_blk, b_own, c_full, ridge_lam):
        k_loc, i_loc, j_loc = x_blk.shape
        cp_rank = b_own.shape[1]
        x_half = x_blk.astype(jnp.bfloat16)
        flat_x = x_half.reshape(k_loc * i_loc, j_loc)
        tube_idx = lax.axis_index("tube")
        b_cols = lax.all_gather(b_own, ("row", "tube"), axis=0, tiled=True)
        gram_b = lax.psum(gram_of(b_own), ALL_AXES)
        for sweep_idx in range(SWEEPS):
            c_blk = lax.dynamic_slice_in_dim(c_full, tube_idx * k_loc, k_loc, 0)
            gram_c = gram_of(c_full)
            u_kir = jnp.dot(flat_x, b_cols.astype(jnp.bfloat16), preferred_element_type=jnp.float32).reshape(k_loc, i_loc, cp_rank)
            part_a = jnp.einsum("kir,kr->ir", u_kir, c_blk, preferred_element_type=jnp.float32, precision=full_prec)
            mtt_a = lax.psum_scatter(part_a, ("col", "tube"), scatter_dimension=0, tiled=True)
            a_own = solve_rows(mtt_a, gram_b * gram_c, ridge_lam)
            gram_a = lax.psum(gram_of(a_own), ALL_AXES)
            a_rows = lax.all_gather(a_own, ("col", "tube"), axis=0, tiled=True)
            v_kjr = jnp.einsum("kij,ir->kjr", x_half, a_rows.astype(jnp.bfloat16), preferred_element_type=jnp.float32)
            part_b = jnp.einsum("kjr,kr->jr", v_kjr, c_blk, preferred_element_type=jnp.float32, precision=full_prec)
            mtt_b = lax.psum_scatter(part_b, ("row", "tube"), scatter_dimension=0, tiled=True)
            b_own = solve_rows(mtt_b, gram_a * gram_c, ridge_lam)
            gram_b = lax.psum(gram_of(b_own), ALL_AXES)
            b_cols = lax.all_gather(b_own, ("row", "tube"), axis=0, tiled=True)
            u_kir = jnp.dot(flat_x, b_cols.astype(jnp.bfloat16), preferred_element_type=jnp.float32).reshape(k_loc, i_loc, cp_rank)
            part_c = jnp.einsum("kir,ir->kr", u_kir, a_rows, preferred_element_type=jnp.float32, precision=full_prec)
            c_local = lax.psum(part_c, ("row", "col"))
            mtt_c = lax.all_gather(c_local, "tube", axis=0, tiled=True)
            c_full = solve_rows(mtt_c, gram_a * gram_b, ridge_lam)
        return a_own, b_own, c_full

    return jax.shard_map(
        local_sweeps,
        mesh=mesh,
        in_specs=(P("tube", "row", "col"), P(("col", "row", "tube"), None), P(None, None), P()),
        out_specs=(P(("row", "col", "tube"), None), P(("col", "row", "tube"), None), P(None, None)),
        check_vma=False,
    )
```

profile of v0, /device:TPU:0, one launch (start us, length us, event | category | flops | bytes accessed | tf_op | source)
XLA Modules:
  0.0 352.1 jit_solution(3015047651000256011)
XLA Ops:
  8.1 10.2 %all_gather.21 = bf16[1024,64]{0,1:T(8,128)(2,1)S(1)} all-gather(bf16[256,64]{0,1:T(8,128)(2,1)S(1)} %convert), channel_id=1, replica_groups=mesh['tube'=2,'col'=2,'row'=2] {'row','tube'}, dimensions={0}, use_global_device_ids=true | all-gather | bytes 163840 | tf_op jit(solution)/shard_map/all_gather | solution.py:31
  18.3 9.1 %convert_element_type.48 = bf16[16,256,1024]{2,1,0:T(8,128)(2,1)} convert(f32[16,256,1024]{2,1,0:T(8,128)} %param.17) | non-fusion elementwise | flops 4194304 | bytes 25165824 | tf_op jit(solution)/shard_map/convert_element_type | solution.py:28
  27.4 6.4 %multiply_reduce_fusion = f32[64,256]{0,1:T(8,128)} fusion(bf16[16,256,1024]{2,1,0:T(8,128)(2,1)} %convert_element_type.48, f32[64,16]{0,1:T(8,128)S(1)} %get-tuple-element.16, bf16[1024,64]{0,1:T(8,128)(2,1)S(1)} %all_gather.21), kind=kOutput, calls=%fused_computation.6 | convolution fusion | flops 537378816 | bytes 8589312 | tf_op jit(solution)/shard_map/dot_general | solution.py:36
  34.8 22.3 %psum.49 = f32[64,64]{0,1:T(8,128)S(1)} all-reduce(f32[64,64]{0,1:T(8,128)S(1)} %fusion.52), channel_id=1, replica_groups=mesh['tube'=2,'col'=2,'row'=2] {'tube','col','row'}, use_global_device_ids=true, to_apply=%region_0.0 | all-reduce | flops 4096 | bytes 32768 | tf_op jit(solution)/shard_map/psum | solution.py:32
  57.4 5.8 %cholesky.104 = f32[64,64]{1,0:T(8,128)S(1)} custom-call(f32[64,64]{1,0:T(8,128)S(1)} %fusion.41), custom_call_target="Cholesky" | custom-call | tf_op jit(solution)/shard_map/jit(cholesky)/cholesky | solution.py:17
  64.6 4.9 %custom-call.27 = f32[1,64,64]{1,2,0:T(8,128)S(1)} custom-call(f32[1,64,64]{2,1,0:T(8,128)S(1)} %fusion.18), custom_call_target="InvertDiagBlocksLowerTriangular" | custom-call | tf_op jit(solution)/shard_map/triangular_solve/custom-call.2 | solution.py:19
  70.9 24.1 %psum.50 = f32[64,64]{0,1:T(8,128)S(1)} all-reduce(f32[64,64]{0,1:T(8,128)S(1)} %fusion.56), channel_id=1, replica_groups=mesh['tube'=2,'col'=2,'row'=2] {'tube','col','row'}, use_global_device_ids=true, to_apply=%region_4.8 | all-reduce | flops 4096 | bytes 32768 | tf_op jit(solution)/shard_map/psum | solution.py:40
  95.2 9.5 %all_gather.22 = f32[256,64]{1,0:T(8,128)S(1)} all-gather(f32[64,64]{1,0:T(8,128)S(1)} %copy.29), channel_id=1, replica_groups=mesh['tube'=2,'col'=2,'row'=2] {'col','tube'}, dimensions={0}, use_global_device_ids=true | all-gather | bytes 81920 | tf_op jit(solution)/shard_map/all_gather | solution.py:41
  104.7 5.0 %fusion.14 = f32[64,16,1024]{2,0,1:T(8,128)S(1)} fusion(bf16[16,256,1024]{2,1,0:T(8,128)(2,1)} %convert_element_type.48, f32[256,64]{1,0:T(8,128)S(1)} %all_gather.22), kind=kOutput, calls=%fused_computation.37 | convolution fusion | flops 536887296 | bytes 12648448 | tf_op jit(solution)/shard_map/kij,ir->kjr/dot_general | solution.py:42
  109.7 4.4 %fusion.2 = f32[64,1,1024]{2,1,0:T(1,128)S(1)} fusion(f32[16,64,1]{0,2,1:T(1,128)S(1)} %copy.52, f32[64,16,1024]{2,0,1:T(8,128)S(1)} %fusion.14), kind=kOutput, calls=%fused_computation.2 | convolution fusion | flops 12582912 | bytes 4460544 | tf_op jit(solution)/shard_map/kjr,kr->jr/dot_general | solution.py:43
  114.9 5.8 %cholesky.115 = f32[64,64]{1,0:T(8,128)S(1)} custom-call(f32[64,64]{1,0:T(8,128)S(1)} %fusion.38), custom_call_target="Cholesky" | custom-call | tf_op jit(solution)/shard_map/jit(cholesky)/cholesky | solution.py:17
  122.1 4.9 %custom-call.29 = f32[1,64,64]{1,2,0:T(8,128)S(1)} custom-call(f32[1,64,64]{2,1,0:T(8,128)S(1)} %fusion.19), custom_call_target="InvertDiagBlocksLowerTriangular" | custom-call | tf_op jit(solution)/shard_map/triangular_solve/custom-call.4 | solution.py:19
  131.1 7.1 %all_gather.23 = bf16[1024,64]{0,1:T(8,128)(2,1)S(1)} all-gather(bf16[256,64]{0,1:T(8,128)(2,1)S(1)} %convolution_bitcast_fusion.2), channel_id=1, replica_groups=mesh['tube'=2,'col'=2,'row'=2] {'row','tube'}, dimensions={0}, use_global_device_ids=true | all-gather | bytes 163840 | tf_op jit(solution)/shard_map/all_gather | solution.py:47
  138.3 24.1 %psum.51 = f32[64,64]{0,1:T(8,128)S(1)} all-reduce(f32[64,64]{0,1:T(8,128)S(1)} %fusion.66), channel_id=1, replica_groups=mesh['tube'=2,'col'=2,'row'=2] {'tube','col','row'}, use_global_device_ids=true, to_apply=%region_6.12 | all-reduce | flops 4096 | bytes 32768 | tf_op jit(solution)/shard_map/psum | solution.py:46
  162.4 5.8 %cholesky.126 = f32[64,64]{1,0:T(8,128)S(1)} custom-call(f32[64,64]{1,0:T(8,128)S(1)} %fusion.35), custom_call_target="Cholesky" | custom-call | tf_op jit(solution)/shard_map/jit(cholesky)/cholesky | solution.py:17
  169.6 4.9 %custom-call.31 = f32[1,64,64]{1,2,0:T(8,128)S(1)} custom-call(f32[1,64,64]{2,1,0:T(8,128)S(1)} %fusion.20), custom_call_target="InvertDiagBlocksLowerTriangular" | custom-call | tf_op jit(solution)/shard_map/triangular_solve/custom-call.6 | solution.py:19
  174.5 6.1 %fusion.65 = f32[64,4096]{1,0:T(8,128)S(1)} fusion(bf16[1024,64]{0,1:T(8,128)(2,1)S(1)} %all_gather.23, bf16[4096,1024]{1,0:T(8,128)(2,1)} %bitcast.189), kind=kOutput, calls=%fused_computation.115 | convolution fusion | flops 536870912 | bytes 9568256 | tf_op jit(solution)/shard_map/dot_general | solution.py:48
  181.2 8.3 %psum.52 = f32[16,64]{1,0:T(8,128)S(1)} all-reduce(f32[16,64]{1,0:T(8,128)S(1)} %bitcast.202), channel_id=1, replica_groups=mesh['tube'=2,'col'=2,'row'=2] {'row','col'}, use_global_device_ids=true, to_apply=%region_7.13 | all-reduce | flops 1024 | bytes 8192 | tf_op jit(solution)/shard_map/psum | solution.py:50
  195.4 5.8 %cholesky.137 = f32[64,64]{1,0:T(8,128)S(1)} custom-call(f32[64,64]{1,0:T(8,128)S(1)} %fusion.32), custom_call_target="Cholesky" | custom-call | tf_op jit(solution)/shard_map/jit(cholesky)/cholesky | solution.py:17
  203.4 4.9 %custom-call.33 = f32[1,64,64]{1,2,0:T(8,128)S(1)} custom-call(f32[1,64,64]{2,1,0:T(8,128)S(1)} %fusion.21), custom_call_target="InvertDiagBlocksLowerTriangular" | custom-call | tf_op jit(solution)/shard_map/triangular_solve/custom-call.2 | solution.py:19
  208.3 13.9 %reduce-scatter.15.cloned.1.call-done = f32[64,64]{1,0:T(8,128)} async-done(((f32[256,64]{1,0:T(8,128)}), f32[64,64]{1,0:T(8,128)}) %reduce-scatter.15.cloned.1.call-update) | async-done | bytes 16400
  223.5 22.3 %psum.53 = f32[64,64]{0,1:T(8,128)S(1)} all-reduce(f32[64,64]{0,1:T(8,128)S(1)} %fusion.54), channel_id=1, replica_groups=mesh['tube'=2,'col'=2,'row'=2] {'tube','col','row'}, use_global_device_ids=true, to_apply=%region_9.17 | all-reduce | flops 4096 | bytes 32768 | tf_op jit(solution)/shard_map/psum | solution.py:40
  246.0 9.4 %all_gather.25 = f32[256,64]{1,0:T(8,128)S(1)} all-gather(f32[64,64]{1,0:T(8,128)S(1)} %copy.40), channel_id=1, replica_groups=mesh['tube'=2,'col'=2,'row'=2] {'col','tube'}, dimensions={0}, use_global_device_ids=true | all-gather | bytes 81920 | tf_op jit(solution)/shard_map/all_gather | solution.py:41
  255.4 5.0 %fusion.12 = f32[64,16,1024]{2,0,1:T(8,128)S(1)} fusion(bf16[16,256,1024]{2,1,0:T(8,128)(2,1)} %convert_element_type.48, f32[256,64]{1,0:T(8,128)S(1)} %all_gather.25), kind=kOutput, calls=%fused_computation.35 | convolution fusion | flops 536887296 | bytes 12648448 | tf_op jit(solution)/shard_map/kij,ir->kjr/dot_general | solution.py:42
  265.6 5.8 %cholesky.148 = f32[64,64]{1,0:T(8,128)S(1)} custom-call(f32[64,64]{1,0:T(8,128)S(1)} %fusion.29), custom_call_target="Cholesky" | custom-call | tf_op jit(solution)/shard_map/jit(cholesky)/cholesky | solution.py:17
  272.7 4.9 %custom-call.35 = f32[1,64,64]{1,2,0:T(8,128)S(1)} custom-call(f32[1,64,64]{2,1,0:T(8,128)S(1)} %fusion.22), custom_call_target="InvertDiagBlocksLowerTriangular" | custom-call | tf_op jit(solution)/shard_map/triangular_solve/custom-call.4 | solution.py:19
  281.8 22.3 %psum.54 = f32[64,64]{0,1:T(8,128)S(1)} all-reduce(f32[64,64]{0,1:T(8,128)S(1)} %fusion.48), channel_id=1, replica_groups=mesh['tube'=2,'col'=2,'row'=2] {'tube','col','row'}, use_global_device_ids=true, to_apply=%region_11.19 | all-reduce | flops 4096 | bytes 32768 | tf_op jit(solution)/shard_map/psum | solution.py:46
  304.3 5.8 %cholesky.159 = f32[64,64]{1,0:T(8,128)S(1)} custom-call(f32[64,64]{1,0:T(8,128)S(1)} %fusion.26), custom_call_target="Cholesky" | custom-call | tf_op jit(solution)/shard_map/jit(cholesky)/cholesky | solution.py:17
  311.5 4.9 %custom-call.37 = f32[1,64,64]{1,2,0:T(8,128)S(1)} custom-call(f32[1,64,64]{2,1,0:T(8,128)S(1)} %fusion.23), custom_call_target="InvertDiagBlocksLowerTriangular" | custom-call | tf_op jit(solution)/shard_map/triangular_solve/custom-call.6 | solution.py:19
  316.4 9.4 %all_gather.26 = bf16[1024,64]{0,1:T(8,128)(2,1)S(1)} all-gather(bf16[256,64]{0,1:T(8,128)(2,1)S(1)} %get-tuple-element.22), channel_id=1, replica_groups=mesh['tube'=2,'col'=2,'row'=2] {'row','tube'}, dimensions={0}, use_global_device_ids=true | all-gather | bytes 163840 | tf_op jit(solution)/shard_map/all_gather | solution.py:47
  325.8 6.0 %fusion.64 = f32[64,4096]{1,0:T(8,128)S(1)} fusion(bf16[1024,64]{0,1:T(8,128)(2,1)S(1)} %all_gather.26, bf16[4096,1024]{1,0:T(8,128)(2,1)} %bitcast.190), kind=kOutput, calls=%fused_computation.114 | convolution fusion | flops 536870912 | bytes 9568256 | tf_op jit(solution)/shard_map/dot_general | solution.py:48
  332.4 7.5 %psum.55 = f32[16,64]{1,0:T(8,128)S(1)} all-reduce(f32[16,64]{1,0:T(8,128)S(1)} %bitcast.203), channel_id=1, replica_groups=mesh['tube'=2,'col'=2,'row'=2] {'row','col'}, use_global_device_ids=true, to_apply=%region_12.20 | all-reduce | flops 1024 | bytes 8192 | tf_op jit(solution)/shard_map/psum | solution.py:50
  (94 shorter events, 40.0 us)
Async XLA Ops:
  7.2 62.4 %reduce-scatter.13.cloned.1.call-start = ((), (), s32[]{:S(2)}) async-start(), calls=%async_computation.6 | async-start | bytes 163840
  18.3 9.1 %copy-start.3 = (f32[32,64]{1,0:T(8,128)S(1)}, f32[32,64]{1,0:T(8,128)}, u32[]{:S(2)}) copy-start(f32[32,64]{1,0:T(8,128)} %param.19) | copy-start | bytes 24580
  27.4 6.5 %copy-start.1 = (f32[256,64]{0,1:T(8,128)S(1)}, f32[256,64]{0,1:T(8,128)}, u32[]{:S(2)}) copy-start(f32[256,64]{0,1:T(8,128)} %param.18) | copy-start | bytes 196612
  33.9 95.8 %reduce-scatter.9.cloned.1.call-start = ((), (), s32[]{:S(2)}) async-start(), calls=%async_computation.4 | async-start | bytes 327680 | tf_op jit(solution)/shard_map/reduce_scatter | solution.py:44
  114.8 107.3 %reduce-scatter.15.cloned.1.call-start = ((), (), s32[]{:S(2)}) async-start(), calls=%async_computation.7 | async-start | bytes 163840
  202.7 77.7 %reduce-scatter.11.cloned.1.call-start = ((), (), s32[]{:S(2)}) async-start(), calls=%async_computation.5 | async-start | bytes 327680 | tf_op jit(solution)/shard_map/reduce_scatter | solution.py:44
  223.4 41.3 %copy-start.2 = (f32[64,64]{1,0:T(8,128)}, f32[64,64]{1,0:T(8,128)S(1)}, u32[]{:S(2)}) copy-start(f32[64,64]{1,0:T(8,128)S(1)} %copy.40) | copy-start | bytes 49156
  281.7 63.7 %copy-start = (f32[256,64]{0,1:T(8,128)}, f32[256,64]{0,1:T(8,128)S(1)}, u32[]{:S(2)}) copy-start(f32[256,64]{0,1:T(8,128)S(1)} %get-tuple-element.23) | copy-start | bytes 196612
Sparse Core Ops, SparseCore 0:
  34.0 18.6 reduce-scatter.12
  115.0 14.6 reduce-scatter.8
  202.8 19.3 reduce-scatter.14
  265.7 14.6 reduce-scatter.10
where the time goes:
time: 358 us; the launch traced here: 352 us
  blocking collectives  185 us (52%)
  other arithmetic  82.9 us (23%)
  matrix products  45.3 us (13%)
  waiting for transfers between devices  19.2 us (5%)
  between operations  15.1 us (4%)
  local copies, waits for them, and re-layouts  4.02 us (1%)
    psum x3, blocking collectives, local_sweeps(): gram_b = lax.psum(gram_of(b_own), ALL_AXES)  68.7 us
    psum x2, blocking collectives, local_sweeps(): gram_a = lax.psum(gram_of(a_own), ALL_AXES)  46.5 us
    another operation x18, other arithmetic, solve_rows(): chol_fac = jnp.linalg.cholesky(gram_prod + ridge_lam * ident_mat)  39.1 us
    another operation x12, other arithmetic, solve_rows(): lax.linalg.triangular_solve(chol_fac, half_solve, left_side=False, lower=...  33.3 us
    all_gather x3, blocking collectives, local_sweeps(): b_cols = lax.all_gather(b_own, ('row', 'tube'), axis=0, tiled=True)  26.7 us
    all_gather x2, blocking collectives, local_sweeps(): a_rows = lax.all_gather(a_own, ('col', 'tube'), axis=0, tiled=True)  18.9 us
    dot_general x3, matrix products, local_sweeps(): jnp.dot(flat_x, b_cols.astype(jnp.bfloat16), preferred_element_type=jnp.f...  18.5 us
    psum x2, blocking collectives, local_sweeps(): c_local = lax.psum(part_c, ('row', 'col'))  15.8 us
  transfers between devices with their start and end apart: 4, of which 3 were waited for; matrix products, arithmetic and copies ran while one was open for 12% of the time, Pallas kernels for 0%

commit v1 on v0

v1 whole, which is shorter than its diff:
```python
import functools

import jax
import jax.numpy as jnp
from jax import lax
from jax.experimental import pallas as pl
from jax.experimental.pallas import tpu as pltpu
from jax.sharding import PartitionSpec as P

SWEEPS = 2
RANK = 64
LANES = 128
K_LOC = 16
I_LOC = 256
J_TILE = 256
J_TILES = 4
I_HALF = I_LOC // 2
A_CHUNKS = 4
A_CHUNK = I_HALF // A_CHUNKS
BLK = 16
MESH = pl.DeviceIdType.MESH
HIGH = lax.Precision.HIGHEST
F32 = jnp.float32
BF16 = jnp.bfloat16


def dot_nn(a, b, precision=None):
    return lax.dot_general(a, b, (((1,), (0,)), ((), ())), precision=precision, preferred_element_type=F32)


def dot_nt(a, b, precision=None):
    return lax.dot_general(a, b, (((1,), (1,)), ((), ())), precision=precision, preferred_element_type=F32)


def dot_tn(a, b, precision=None):
    return lax.dot_general(a, b, (((0,), (0,)), ((), ())), precision=precision, preferred_element_type=F32)


def inverse_quad(gram_dup, lam):
    row_ids = lax.broadcasted_iota(jnp.int32, (RANK, LANES), 0)
    lane_ids = lax.broadcasted_iota(jnp.int32, (RANK, LANES), 1)
    left_eye = jnp.where(lane_ids == row_ids, 1.0, 0.0).astype(F32)
    right_eye = jnp.where(lane_ids == row_ids + RANK, 1.0, 0.0).astype(F32)
    aug = jnp.where(lane_ids < RANK, gram_dup + lam * left_eye, right_eye)
    n_blk = RANK // BLK
    blocks = [aug[b * BLK:(b + 1) * BLK] for b in range(n_blk)]
    sub_ids = lax.broadcasted_iota(jnp.int32, (BLK, LANES), 0)
    done = []
    for b in range(n_blk):
        piv = blocks[b]
        cols = [jnp.broadcast_to(piv[:, b * BLK + c:b * BLK + c + 1], (BLK, LANES)) for c in range(BLK)]
        mults = [[jnp.broadcast_to(blocks[t][:, b * BLK + c:b * BLK + c + 1], (BLK, LANES)) for c in range(BLK)]
                 for t in range(b + 1, n_blk)]
        chol_rows = jnp.zeros((BLK, LANES), F32)
        for c in range(BLK):
            is_row = sub_ids == c
            root = lax.rsqrt(jnp.broadcast_to(cols[c][c:c + 1, :], (BLK, LANES)))
            scaled_col = cols[c] * root
            scaled_row = jnp.broadcast_to(piv[c:c + 1, :], (BLK, LANES)) * root
            chol_rows = jnp.where(is_row, scaled_row, chol_rows)
            piv = jnp.where(is_row, scaled_row * root, piv - scaled_col * scaled_row)
            for c2 in range(c + 1, BLK):
                scaled_elt = jnp.broadcast_to(cols[c2][c:c + 1, :], (BLK, LANES)) * root
                cols[c2] = jnp.where(is_row, scaled_elt * root, cols[c2] - scaled_col * scaled_elt)
        done.append(chol_rows)
        for t in range(b + 1, n_blk):
            upd = blocks[t]
            for c in range(BLK):
                upd = upd - mults[t - b - 1][c] * jnp.broadcast_to(piv[c:c + 1, :], (BLK, LANES))
            blocks[t] = upd
    chol = jnp.concatenate(done, axis=0)
    inv_dup = jnp.where(lane_ids < RANK, pltpu.roll(chol, RANK, 1), chol)
    return dot_tn(inv_dup, inv_dup, HIGH)


def kernel(x_hbm, b_init, c_init, lam_ref, a_out, b_out, c_out,
           xf, x4, u_ref, bd, bpk, brcv, cd, cb, a_ref, at_ref,
           ma_snd, ma_rcv, ga_snd, ga_rcv, mb_snd, mb_d2d, mb_sum, mb_rcv, bo_ref,
           gb_snd, gb_rcv, gb_all, mc_snd, mc_rcv, mc_all,
           x_sem, b_ss, b_rs, ma_ss, ma_rs, ga_ss, ga_rs, md_ss, md_rs, my_ss, my_rs,
           ag_ss, ag_rs, gb_ss, gb_rs, mc_ss, mc_rs):
    tube, col, row = lax.axis_index("tube"), lax.axis_index("col"), lax.axis_index("row")

    def peer(d):
        t = 1 - tube if d & 4 else tube
        c = 1 - col if d & 2 else col
        r = 1 - row if d & 1 else row
        return (t, c, r)

    def send(src, dst, ss, rs, d):
        return pltpu.make_async_remote_copy(src_ref=src, dst_ref=dst, send_sem=ss, recv_sem=rs,
                                            device_id=peer(d), device_id_type=MESH)

    def load(k):
        return pltpu.make_async_copy(x_hbm.at[k], xf.at[k], x_sem.at[k])

    @pl.loop(0, K_LOC)
    def _(k):
        load(k).start()

    barrier = pltpu.get_barrier_semaphore()
    for d in range(1, 8):
        pl.semaphore_signal(barrier, inc=1, device_id=peer(d), device_id_type=MESH)

    lam = lam_ref[0, 0]
    lanes_b = lax.broadcasted_iota(jnp.int32, (I_HALF, LANES), 1)
    low_half = lanes_b < RANK
    b_own = b_init[...]
    b_lo, b_hi = b_own[:I_HALF], b_own[I_HALF:]
    bpk[...] = jnp.concatenate([b_lo, b_hi], axis=1).astype(BF16)
    cd[...] = jnp.concatenate([c_init[...], c_init[...]], axis=1)
    pl.semaphore_wait(barrier, 7)

    gather = [(5, 0), (4, 1), (1, 2)]
    copies = [send(bpk, brcv.at[n], b_ss.at[n], b_rs.at[n], d) for d, n in gather]
    for cp in copies:
        cp.start()

    def unpack_b(packed, tile):
        wide = packed.astype(F32)
        turned = pltpu.roll(wide, RANK, 1)
        bd[0, tile, 0:I_HALF, :] = jnp.where(low_half, wide, turned).astype(BF16)
        bd[0, tile, I_HALF:, :] = jnp.where(low_half, turned, wide).astype(BF16)

    unpack_b(bpk[...], row * 2 + tube)
    for (d, n), cp in zip(gather, copies):
        cp.wait()
        t2 = 1 - tube if d & 4 else tube
        r2 = 1 - row if d & 1 else row
        unpack_b(brcv[n], r2 * 2 + t2)

    def gram_b_start(slot):
        gram = jnp.zeros((LANES, LANES), F32)
        for jt in range(J_TILES):
            tile = bd[slot, jt]
            gram = gram + dot_tn(tile, tile)
        gb_snd[slot] = gram[:RANK]
        cp = send(gb_snd.at[slot], gb_rcv.at[slot], gb_ss.at[slot], gb_rs.at[slot], 2)
        cp.start()

    def gram_b_finish(slot):
        send(gb_snd.at[slot], gb_rcv.at[slot], gb_ss.at[slot], gb_rs.at[slot], 2).wait()
        gb_all[...] = gb_snd[slot] + gb_rcv[slot]

    def pack_u(u_both):
        return jnp.where(low_half, u_both[:I_HALF], u_both[I_HALF:])

    gram_b_start(0)

    @pl.loop(0, K_LOC)
    def _(k):
        load(k).wait()
        u_both = jnp.zeros((I_LOC, LANES), F32)
        for jt in range(J_TILES):
            xb = xf[k, :, jt * J_TILE:(jt + 1) * J_TILE].astype(BF16)
            x4[jt, k] = xb
            u_both = u_both + dot_nn(xb, bd[0, jt])
        u_ref[k] = pack_u(u_both)

    gram_b_finish(0)

    @pl.loop(0, SWEEPS)
    def _(s):
        k_base = pl.multiple_of(tube * K_LOC, K_LOC)
        c_own = cd[pl.ds(k_base, K_LOC), :]
        a_copies = []
        for ch in range(A_CHUNKS):
            rows = pl.ds(ch * A_CHUNK, A_CHUNK)
            part = jnp.zeros((A_CHUNK, LANES), F32)
            for k in range(K_LOC):
                part = part + u_ref[k, ch * A_CHUNK:(ch + 1) * A_CHUNK, :] * c_own[k:k + 1, :]
            ma_snd[ch * A_CHUNK:(ch + 1) * A_CHUNK, :] = part
            for n, d in ((2, 6), (1, 4), (0, 2)):
                cp = send(ma_snd.at[rows], ma_rcv.at[s, n, rows], ma_ss.at[n, ch], ma_rs.at[s, n, ch], d)
                cp.start()
                a_copies.append(cp)
        c_half = cd[...].astype(BF16)
        gram_c = dot_tn(c_half, c_half)[:RANK]
        c_turn = c_own.T
        for k in range(K_LOC):
            cb[k] = jnp.broadcast_to(c_turn[:RANK, k:k + 1], (RANK, LANES))
        inv_a = inverse_quad(gb_all[...] * gram_c, lam)
        quad_r = lax.broadcasted_iota(jnp.int32, (LANES, LANES), 0) < RANK
        quad_c = lax.broadcasted_iota(jnp.int32, (LANES, LANES), 1) < RANK
        inv_diag = jnp.where(quad_r == quad_c, inv_a, 0.0)
        for cp in a_copies:
            cp.wait()
        mtt_a = (ma_snd[...] + ma_rcv[s, 0]) + (ma_rcv[s, 1] + ma_rcv[s, 2])
        a_new = dot_nn(mtt_a, inv_diag, HIGH)
        a_ref[...] = a_new
        a_turn = a_new.T.astype(BF16)
        at_ref[:, :I_HALF] = a_turn[:RANK]
        at_ref[:, I_HALF:] = a_turn[RANK:]
        at = at_ref[...]
        ga_snd[...] = dot_nt(at, jnp.concatenate([at, at], axis=0))
        ga_cp = send(ga_snd, ga_rcv.at[s], ga_ss, ga_rs.at[s], 1)
        ga_cp.start()

        def v_tile(jt):
            acc = jnp.zeros((RANK, J_TILE), F32)
            for k in range(K_LOC):
                v_kt = dot_nn(at_ref[...], x4[jt, k])
                c_col = cb[k]
                acc = acc + v_kt * jnp.concatenate([c_col, c_col], axis=1)
            return acc

        d_copies = []
        for q in range(2):
            mb_snd[q] = v_tile((1 - row) * 2 + q)
            cp = send(mb_snd.at[q], mb_d2d.at[s, q], md_ss.at[q], md_rs.at[s, q], 1)
            cp.start()
            d_copies.append(cp)
        y_copies = []
        for q in range(2):
            own = v_tile(row * 2 + q)
            d_copies[q].wait()
            mb_sum[q] = own + mb_d2d[s, q]
            cp = send(mb_sum.at[q], mb_rcv.at[s, q], my_ss.at[q], my_rs.at[s, q], 4)
            cp.start()
            y_copies.append(cp)
        ga_cp.wait()
        gram_a = ga_snd[...] + ga_rcv[s]
        inv_b = inverse_quad(gram_a * gram_c, lam)
        g_copies = []
        for q in range(2):
            y_copies[q].wait()
            mtt_b = mb_sum[q] + mb_rcv[s, q]
            b_new = dot_tn(mtt_b, inv_b[:RANK], HIGH)
            bo_ref[q] = b_new
            tile = bd.at[s + 1, row * 2 + q]
            tile[...] = b_new.astype(BF16)
            cp = send(tile, tile, ag_ss.at[q], ag_rs.at[s, q], 1)
            cp.start()
            g_copies.append(cp)
        for cp in g_copies:
            cp.wait()

        gram_b_start(s + 1)

        @pl.loop(0, K_LOC)
        def _(k):
            u_both = jnp.zeros((I_LOC, LANES), F32)
            for jt in range(J_TILES):
                u_both = u_both + dot_nn(x4[jt, k], bd[s + 1, jt])
            u_new = pack_u(u_both)
            u_ref[k] = u_new
            mc_snd[pl.ds(k, 1), :] = jnp.sum(u_new * a_ref[...], axis=0, keepdims=True)

        c_copies = []
        for d in (7, 6, 5, 4, 3, 2, 1):
            cp = send(mc_snd, mc_rcv.at[s, d - 1], mc_ss.at[d - 1], mc_rs.at[s, d - 1], d)
            cp.start()
            c_copies.append(cp)
        gram_b_finish(s + 1)
        inv_c = inverse_quad(gram_a * gb_all[...], lam)
        for cp in c_copies:
            cp.wait()
        near = (mc_snd[...] + mc_rcv[s, 0]) + (mc_rcv[s, 1] + mc_rcv[s, 2])
        far = (mc_rcv[s, 3] + mc_rcv[s, 4]) + (mc_rcv[s, 5] + mc_rcv[s, 6])
        mc_all[pl.ds(k_base, K_LOC), :] = near
        mc_all[pl.ds(pl.multiple_of((1 - tube) * K_LOC, K_LOC), K_LOC), :] = far
        cd[...] = dot_nn(mc_all[...], inv_c, HIGH)

    a_rows = a_ref[pl.ds(pl.multiple_of(tube * RANK, RANK), RANK), :]
    a_out[...] = jnp.where(col == 0, a_rows[:, :RANK], a_rows[:, RANK:])
    b_out[...] = bo_ref[tube][:, :RANK]
    c_out[...] = cd[:, :RANK]


def solution(mesh):
    def local(x_blk, b_own, c_full, ridge_lam):
        dma = pltpu.SemaphoreType.DMA
        vm = pltpu.VMEM
        return pl.pallas_call(
            kernel,
            out_shape=(jax.ShapeDtypeStruct((64, RANK), F32), jax.ShapeDtypeStruct((256, RANK), F32),
                       jax.ShapeDtypeStruct((32, RANK), F32)),
            in_specs=[pl.BlockSpec(memory_space=pl.ANY), pl.BlockSpec(memory_space=pltpu.VMEM),
                      pl.BlockSpec(memory_space=pltpu.VMEM), pl.BlockSpec(memory_space=pltpu.SMEM)],
            out_specs=(pl.BlockSpec(memory_space=pltpu.VMEM),) * 3,
            scratch_shapes=[
                vm((K_LOC, I_LOC, J_TILE * J_TILES), F32),
                vm((J_TILES, K_LOC, I_LOC, J_TILE), BF16),
                vm((K_LOC, I_HALF, LANES), F32),
                vm((SWEEPS + 1, J_TILES, J_TILE, LANES), BF16),
                vm((I_HALF, LANES), BF16),
                vm((3, I_HALF, LANES), BF16),
                vm((2 * K_LOC, LANES), F32),
                vm((K_LOC, RANK, LANES), F32),
                vm((I_HALF, LANES), F32),
                vm((RANK, I_LOC), BF16),
                vm((I_HALF, LANES), F32),
                vm((SWEEPS, 3, I_HALF, LANES), F32),
                vm((RANK, LANES), F32),
                vm((SWEEPS, RANK, LANES), F32),
                vm((2, RANK, J_TILE), F32),
                vm((SWEEPS, 2, RANK, J_TILE), F32),
                vm((2, RANK, J_TILE), F32),
                vm((SWEEPS, 2, RANK, J_TILE), F32),
                vm((2, J_TILE, LANES), F32),
                vm((SWEEPS + 1, RANK, LANES), F32),
                vm((SWEEPS + 1, RANK, LANES), F32),
                vm((RANK, LANES), F32),
                vm((K_LOC, LANES), F32),
                vm((SWEEPS, 7, K_LOC, LANES), F32),
                vm((2 * K_LOC, LANES), F32),
                dma((K_LOC,)), dma((3,)), dma((3,)),
                dma((3, A_CHUNKS)), dma((SWEEPS, 3, A_CHUNKS)),
                dma, dma((SWEEPS,)),
                dma((2,)), dma((SWEEPS, 2)), dma((2,)), dma((SWEEPS, 2)),
                dma((2,)), dma((SWEEPS, 2)),
                dma((SWEEPS + 1,)), dma((SWEEPS + 1,)),
                dma((7,)), dma((SWEEPS, 7)),
            ],
            compiler_params=pltpu.CompilerParams(collective_id=0, has_side_effects=True,
                                                 vmem_limit_bytes=60 * 1024 * 1024),
            name="als_sweeps",
        )(x_blk, b_own, c_full, ridge_lam.reshape(1, 1))

    return jax.shard_map(
        local,
        mesh=mesh,
        in_specs=(P("tube", "row", "col"), P(("col", "row", "tube"), None), P(None, None), P()),
        out_specs=(P(("row", "col", "tube"), None), P(("col", "row", "tube"), None), P(None, None)),
        check_vma=False,
    )
```

time: 358 us -> 65.4 us (0.18); the launches traced: 352 us -> 65.1 us
  blocking collectives: 185 us -> 0 us
  other arithmetic: 82.9 us -> 0 us
  Pallas kernels: 0 us -> 57.9 us
  matrix products: 45.3 us -> 0 us
  waiting for transfers between devices: 19.2 us -> 0 us
  between operations: 15.1 us -> 1.29 us
    psum x7 -> x0, blocking collectives: 131 us -> none  [the longest x3 68.7 us: local_sweeps(): gram_b = lax.psum(gram_of(b_own), ALL_AXES)]
    another operation x30 -> x0, other arithmetic: 72.4 us -> none  [the longest x18 39.1 us: solve_rows(): chol_fac = jnp.linalg.cholesky(gram_prod + ridge_lam * ident_mat)]
    pallas_call x0 -> x1, Pallas kernels: none -> 57.9 us  [local(): pl.pallas_call(kernel, out_shape=(jax.ShapeDtypeStruct((64, RANK), F32),...]
    all_gather x7 -> x0, blocking collectives: 54.3 us -> none  [the longest x3 26.7 us: local_sweeps(): b_cols = lax.all_gather(b_own, ('row', 'tube'), axis=0, tiled=True)]
    dot_general x15 -> x0, matrix products: 38.9 us -> none  [the longest x3 18.5 us: local_sweeps(): jnp.dot(flat_x, b_cols.astype(jnp.bfloat16), preferred_element_type=jnp.f...]
    unnamed x6 -> x0, waiting for transfers between devices: 14 us -> none
    convert_element_type x1 -> x0, other arithmetic: 9.12 us -> none  [local_sweeps(): x_half = x_blk.astype(jnp.bfloat16)]
    another operation x12 -> x0, matrix products: 6.39 us -> none  [the longest x6 4.62 us: solve_rows(): lax.linalg.triangular_solve(chol_fac, mttkrp_rows, left_side=False, lower...]
  transfers between devices with their start and end apart: 4 -> 0, of which waited for: 3 -> 0; matrix products, arithmetic and copies ran while one was open for 12% -> 0% of each run, Pallas kernels for 0% -> 0%
where the time goes in v1:
time: 65.4 us; the launch traced here: 65.1 us
  Pallas kernels  57.9 us (89%)
  local copies, waits for them, and re-layouts  5.9 us (9%)
  between operations  1.29 us (2%)
    pallas_call x1, Pallas kernels, local(): pl.pallas_call(kernel, out_shape=(jax.ShapeDtypeStruct((64, RANK), F32),...  57.9 us
    unnamed x3, local copies, waits for them, and re-layouts  4.29 us
    pallas_call x1, local copies, waits for them, and re-layouts, local(): pl.pallas_call(kernel, out_shape=(jax.ShapeDtypeStruct((64, RANK), F32),...  1.62 us

profile of v1, /device:TPU:0, one launch (start us, length us, event | category | flops | bytes accessed | tf_op | source)
XLA Modules:
  0.0 65.1 jit_solution(2056186846502564533)
XLA Ops:
  1.3 1.6 %copy.7.b_init = f32[256,64]{1,0:T(8,128)} copy(f32[256,64]{0,1:T(8,128)} %param.5) | data formatting | bytes 131072 | tf_op args[1]
  2.9 57.9 %als_sweeps.1 = (f32[64,64]{1,0:T(8,128)}, f32[256,64]{1,0:T(8,128)}, f32[32,64]{1,0:T(8,128)}) custom-call(f32[16,256,1024]{2,1,0:T(8,128)} %x_hbm.1, f32[256,64]{1,0:T(8,128)} %copy.7.b_init, f32[32,64]{1,0:T(8,128)} %c_init.1, f32[1,1]{1,0:T(1,128)} %bitcast.1.lam_ref), custom_call_target="tpu_custom_call" | custom-call | tf_op jit(solution)/shard_map/als_sweeps/pallas_call | solution.py:274
  60.8 1.6 %copy.8 = f32[256,64]{0,1:T(8,128)} copy(f32[256,64]{1,0:T(8,128)} %get-tuple-element.4) | data formatting | bytes 131072 | tf_op jit(solution)/shard_map/als_sweeps/pallas_call | solution.py:274
  62.4 1.4 %copy.12 = f32[64,64]{1,0:T(8,128)} copy(f32[64,64]{1,0:T(8,128)} %get-tuple-element.9) | data formatting | bytes 32768
  63.7 1.3 %copy.13 = f32[32,64]{1,0:T(8,128)} copy(f32[32,64]{1,0:T(8,128)} %get-tuple-element.11) | data formatting | bytes 16384

commit v2 on v1

--- a/solution.py
+++ b/solution.py
@@ -18,6 +18,7 @@
 A_CHUNKS = 4
 A_CHUNK = I_HALF // A_CHUNKS
 BLK = 16
+LOAD_K = 4
 MESH = pl.DeviceIdType.MESH
 HIGH = lax.Precision.HIGHEST
 F32 = jnp.float32
@@ -73,12 +74,12 @@
     return dot_tn(inv_dup, inv_dup, HIGH)
 
 
-def kernel(x_hbm, b_init, c_init, lam_ref, a_out, b_out, c_out,
-           xf, x4, u_ref, bd, bpk, brcv, cd, cb, a_ref, at_ref,
+def kernel(x_hbm, b_hbm, c_hbm, lam_ref, a_out, b_out, c_out,
+           b_init, c_init, xf, x4, u_ref, bd, bpk, brcv, cd, cb, a_ref, at_ref,
            ma_snd, ma_rcv, ga_snd, ga_rcv, mb_snd, mb_d2d, mb_sum, mb_rcv, bo_ref,
-           gb_snd, gb_rcv, gb_all, mc_snd, mc_rcv, mc_all,
-           x_sem, b_ss, b_rs, ma_ss, ma_rs, ga_ss, ga_rs, md_ss, md_rs, my_ss, my_rs,
-           ag_ss, ag_rs, gb_ss, gb_rs, mc_ss, mc_rs):
+           g0_snd, g0_rcv, gb_snd, gb_rcv, gb_all, mc_full, mc_snd, mc_rcv, inv_ref,
+           in_sem, x_sem, b_ss, b_rs, ma_ss, ma_rs, ga_ss, ga_rs, md_ss, md_rs, my_ss, my_rs,
+           ag_ss, ag_rs, g0_ss, g0_rs, gb_ss, gb_rs, mc_ss, mc_rs):
     tube, col, row = lax.axis_index("tube"), lax.axis_index("col"), lax.axis_index("row")
 
     def peer(d):
@@ -91,13 +92,25 @@
         return pltpu.make_async_remote_copy(src_ref=src, dst_ref=dst, send_sem=ss, recv_sem=rs,
                                             device_id=peer(d), device_id_type=MESH)
 
-    def load(k):
-        return pltpu.make_async_copy(x_hbm.at[k], xf.at[k], x_sem.at[k])
-
-    @pl.loop(0, K_LOC)
-    def _(k):
-        load(k).start()
-
+    def load(n, g):
+        rows = pl.ds(g * LOAD_K, LOAD_K)
+        return pltpu.make_async_copy(x_hbm.at[rows, :, pl.ds(pl.multiple_of(tile_of(n) * J_TILE, J_TILE), J_TILE)],
+                                     xf.at[n, rows], x_sem.at[n, g])
+
+    def tile_of(n):
+        r = 1 - row if n & 1 else row
+        t = 1 - tube if n & 2 else tube
+        return r * 2 + t
+
+    small = [pltpu.make_async_copy(b_hbm, b_init, in_sem.at[0]), pltpu.make_async_copy(c_hbm, c_init, in_sem.at[1])]
+    for cp in small:
+        cp.start()
+
+    def load_start(n):
+        for g in range(K_LOC // LOAD_K):
+            load(n, g).start()
+
+    load_start(0)
     barrier = pltpu.get_barrier_semaphore()
     for d in range(1, 8):
         pl.semaphore_signal(barrier, inc=1, device_id=peer(d), device_id_type=MESH)
@@ -105,63 +118,110 @@
     lam = lam_ref[0, 0]
     lanes_b = lax.broadcasted_iota(jnp.int32, (I_HALF, LANES), 1)
     low_half = lanes_b < RANK
-    b_own = b_init[...]
-    b_lo, b_hi = b_own[:I_HALF], b_own[I_HALF:]
-    bpk[...] = jnp.concatenate([b_lo, b_hi], axis=1).astype(BF16)
+    for cp in small:
+        cp.wait()
+    for n in range(1, J_TILES):
+        load_start(n)
+    b_turn = b_init[...]
+    bpk[...] = jnp.concatenate([b_turn[:, :I_HALF], b_turn[:, I_HALF:]], axis=0).T.astype(BF16)
     cd[...] = jnp.concatenate([c_init[...], c_init[...]], axis=1)
     pl.semaphore_wait(barrier, 7)
 
-    gather = [(5, 0), (4, 1), (1, 2)]
-    copies = [send(bpk, brcv.at[n], b_ss.at[n], b_rs.at[n], d) for d, n in gather]
-    for cp in copies:
-        cp.start()
-
-    def unpack_b(packed, tile):
+    def b_send(n):
+        return send(bpk, brcv.at[n - 1], b_ss.at[n - 1], b_rs.at[n - 1], (n & 1) | (n & 2) << 1)
+
+    for n in (3, 2, 1):
+        b_send(n).start()
+
+    def unpack_b(packed, n):
         wide = packed.astype(F32)
         turned = pltpu.roll(wide, RANK, 1)
+        tile = tile_of(n)
         bd[0, tile, 0:I_HALF, :] = jnp.where(low_half, wide, turned).astype(BF16)
         bd[0, tile, I_HALF:, :] = jnp.where(low_half, turned, wide).astype(BF16)
 
-    unpack_b(bpk[...], row * 2 + tube)
-    for (d, n), cp in zip(gather, copies):
-        cp.wait()
-        t2 = 1 - tube if d & 4 else tube
-        r2 = 1 - row if d & 1 else row
-        unpack_b(brcv[n], r2 * 2 + t2)
-
-    def gram_b_start(slot):
-        gram = jnp.zeros((LANES, LANES), F32)
-        for jt in range(J_TILES):
-            tile = bd[slot, jt]
-            gram = gram + dot_tn(tile, tile)
-        gb_snd[slot] = gram[:RANK]
-        cp = send(gb_snd.at[slot], gb_rcv.at[slot], gb_ss.at[slot], gb_rs.at[slot], 2)
-        cp.start()
-
-    def gram_b_finish(slot):
-        send(gb_snd.at[slot], gb_rcv.at[slot], gb_ss.at[slot], gb_rs.at[slot], 2).wait()
-        gb_all[...] = gb_snd[slot] + gb_rcv[slot]
+    half_lanes = lax.broadcasted_iota(jnp.int32, (RANK // 2, LANES), 1) < RANK
+
+    def gram_pack(tiles):
+        gram = sum(dot_tn(tile, tile)[:RANK] for tile in tiles)
+        return jnp.where(half_lanes, gram[:RANK // 2], gram[RANK // 2:])
+
+    def gram_unpack(packed):
+        turned = pltpu.roll(packed, RANK, 1)
+        return jnp.concatenate([jnp.where(half_lanes, packed, turned), jnp.where(half_lanes, turned, packed)], axis=0)
+
+    def g0_send(d):
+        return send(g0_snd, g0_rcv.at[d - 1], g0_ss.at[d - 1], g0_rs.at[d - 1], d)
+
+    def gb_send(s, d):
+        return send(gb_snd, gb_rcv.at[s, d - 1], gb_ss.at[d - 1], gb_rs.at[s, d - 1], d)
+
+    def gram_b_start(s):
+        gb_snd[...] = gram_pack([bd[s + 1, row * 2], bd[s + 1, row * 2 + 1]])
+        for d in (3, 2, 1):
+            gb_send(s, d).start()
+
+    def gram_b_finish(s):
+        for d in (3, 2, 1):
+            gb_send(s, d).wait()
+        gb_all[...] = gram_unpack((gb_snd[...] + gb_rcv[s, 0]) + (gb_rcv[s, 1] + gb_rcv[s, 2]))
 
     def pack_u(u_both):
         return jnp.where(low_half, u_both[:I_HALF], u_both[I_HALF:])
 
-    gram_b_start(0)
-
-    @pl.loop(0, K_LOC)
-    def _(k):
-        load(k).wait()
-        u_both = jnp.zeros((I_LOC, LANES), F32)
-        for jt in range(J_TILES):
-            xb = xf[k, :, jt * J_TILE:(jt + 1) * J_TILE].astype(BF16)
-            x4[jt, k] = xb
-            u_both = u_both + dot_nn(xb, bd[0, jt])
-        u_ref[k] = pack_u(u_both)
-
-    gram_b_finish(0)
+    def u_pass(slot, tiles, first, last, staged=None):
+        for k in range(K_LOC):
+            u_both = jnp.zeros((I_LOC, LANES), F32)
+            for jt in tiles:
+                if staged is None:
+                    x_tile = x4[jt, k]
+                else:
+                    x_tile = xf[staged, k].astype(BF16)
+                    x4[jt, k] = x_tile
+                u_both = u_both + dot_nn(x_tile, bd[slot, jt])
+            u_new = pack_u(u_both)
+            if not first:
+                u_new = u_ref[k] + u_new
+            u_ref[k] = u_new
+            if last:
+                mc_full[k:k + 1, :] = jnp.sum(u_new * a_ref[...], axis=0, keepdims=True)
+
+    unpack_b(bpk[...], 0)
+    g0_snd[...] = gram_pack([bd[0, tile_of(0)]])
+    for d in (7, 6, 3, 2, 5, 4, 1):
+        g0_send(d).start()
+    for n in range(J_TILES):
+        if n > 0:
+            b_send(n).wait()
+            unpack_b(brcv[n - 1], n)
+        for g in range(K_LOC // LOAD_K):
+            load(n, g).wait()
+        u_pass(0, [tile_of(n)], n == 0, False, staged=n)
+    for d in range(1, 8):
+        g0_send(d).wait()
+    here = (g0_snd[...] + g0_rcv[0]) + (g0_rcv[3] + g0_rcv[4])
+    there = (g0_rcv[1] + g0_rcv[2]) + (g0_rcv[5] + g0_rcv[6])
+    gb_all[...] = gram_unpack(here + there)
+
+    k_base = pl.multiple_of(tube * K_LOC, K_LOC)
+    k_far = pl.multiple_of((1 - tube) * K_LOC, K_LOC)
+
+    def c_send(s, d):
+        return send(mc_snd, mc_rcv.at[s, d - 1], mc_ss.at[d - 1], mc_rs.at[s, d - 1], d)
+
+    def c_solve(packed):
+        low = lax.broadcasted_iota(jnp.int32, packed.shape, 1) < RANK
+        split = jnp.concatenate([jnp.where(low, packed, 0.0), jnp.where(low, 0.0, packed)], axis=0)
+        return dot_nn(split, inv_ref[...], HIGH)
+
+    def c_far(s):
+        for d in (4, 5, 6, 7):
+            c_send(s, d).wait()
+        far = (mc_rcv[s, 3] + mc_rcv[s, 4]) + (mc_rcv[s, 5] + mc_rcv[s, 6])
+        cd[pl.ds(k_far, K_LOC), :] = c_solve(far)
 
     @pl.loop(0, SWEEPS)
     def _(s):
-        k_base = pl.multiple_of(tube * K_LOC, K_LOC)
         c_own = cd[pl.ds(k_base, K_LOC), :]
         a_copies = []
         for ch in range(A_CHUNKS):
@@ -174,6 +234,10 @@
                 cp = send(ma_snd.at[rows], ma_rcv.at[s, n, rows], ma_ss.at[n, ch], ma_rs.at[s, n, ch], d)
                 cp.start()
                 a_copies.append(cp)
+        @pl.when(s > 0)
+        def _():
+            c_far(s - 1)
+
         c_half = cd[...].astype(BF16)
         gram_c = dot_tn(c_half, c_half)[:RANK]
         c_turn = c_own.T
@@ -191,10 +255,6 @@
         a_turn = a_new.T.astype(BF16)
         at_ref[:, :I_HALF] = a_turn[:RANK]
         at_ref[:, I_HALF:] = a_turn[RANK:]
-        at = at_ref[...]
-        ga_snd[...] = dot_nt(at, jnp.concatenate([at, at], axis=0))
-        ga_cp = send(ga_snd, ga_rcv.at[s], ga_ss, ga_rs.at[s], 1)
-        ga_cp.start()
 
         def v_tile(jt):
             acc = jnp.zeros((RANK, J_TILE), F32)
@@ -210,6 +270,11 @@
             cp = send(mb_snd.at[q], mb_d2d.at[s, q], md_ss.at[q], md_rs.at[s, q], 1)
             cp.start()
             d_copies.append(cp)
+            if q == 0:
+                at = at_ref[...]
+                ga_snd[...] = dot_nt(at, jnp.concatenate([at, at], axis=0))
+                ga_cp = send(ga_snd, ga_rcv.at[s], ga_ss, ga_rs.at[s], 1)
+                ga_cp.start()
         y_copies = []
         for q in range(2):
             own = v_tile(row * 2 + q)
@@ -222,64 +287,71 @@
         gram_a = ga_snd[...] + ga_rcv[s]
         inv_b = inverse_quad(gram_a * gram_c, lam)
         g_copies = []
-        for q in range(2):
+
+        def b_solve(q):
             y_copies[q].wait()
-            mtt_b = mb_sum[q] + mb_rcv[s, q]
-            b_new = dot_tn(mtt_b, inv_b[:RANK], HIGH)
+            b_new = dot_tn(mb_sum[q] + mb_rcv[s, q], inv_b[:RANK], HIGH)
             bo_ref[q] = b_new
             tile = bd.at[s + 1, row * 2 + q]
             tile[...] = b_new.astype(BF16)
             cp = send(tile, tile, ag_ss.at[q], ag_rs.at[s, q], 1)
             cp.start()
             g_copies.append(cp)
-        for cp in g_copies:
-            cp.wait()
-
-        gram_b_start(s + 1)
-
-        @pl.loop(0, K_LOC)
-        def _(k):
-            u_both = jnp.zeros((I_LOC, LANES), F32)
-            for jt in range(J_TILES):
-                u_both = u_both + dot_nn(x4[jt, k], bd[s + 1, jt])
-            u_new = pack_u(u_both)
-            u_ref[k] = u_new
-            mc_snd[pl.ds(k, 1), :] = jnp.sum(u_new * a_ref[...], axis=0, keepdims=True)
-
-        c_copies = []
-        for d in (7, 6, 5, 4, 3, 2, 1):
-            cp = send(mc_snd, mc_rcv.at[s, d - 1], mc_ss.at[d - 1], mc_rs.at[s, d - 1], d)
-            cp.start()
-            c_copies.append(cp)
-        gram_b_finish(s + 1)
-        inv_c = inverse_quad(gram_a * gb_all[...], lam)
-        for cp in c_copies:
-            cp.wait()
+
+        b_solve(0)
+        u_pass(s + 1, [row * 2], True, False)
+        b_solve(1)
+        gram_b_start(s)
+        g_copies[0].wait()
+        u_pass(s + 1, [row * 2 + 1, (1 - row) * 2], False, False)
+        g_copies[1].wait()
+        u_pass(s + 1, [(1 - row) * 2 + 1], False, True)
+
+        part_c = mc_full[...]
+        part_c = part_c + pltpu.roll(part_c, RANK, 1)
+        low_c = lax.broadcasted_iota(jnp.int32, (K_LOC // 2, LANES), 1) < RANK
+        mc_snd[...] = jnp.where(low_c, part_c[:K_LOC // 2], part_c[K_LOC // 2:])
+        for d in (2, 3, 1, 6, 7, 4, 5):
+            c_send(s, d).start()
+        gram_b_finish(s)
+        inv_ref[...] = inverse_quad(gram_a * gb_all[...], lam)
+        for d in (1, 2, 3):
+            c_send(s, d).wait()
         near = (mc_snd[...] + mc_rcv[s, 0]) + (mc_rcv[s, 1] + mc_rcv[s, 2])
-        far = (mc_rcv[s, 3] + mc_rcv[s, 4]) + (mc_rcv[s, 5] + mc_rcv[s, 6])
-        mc_all[pl.ds(k_base, K_LOC), :] = near
-        mc_all[pl.ds(pl.multiple_of((1 - tube) * K_LOC, K_LOC), K_LOC), :] = far
-        cd[...] = dot_nn(mc_all[...], inv_c, HIGH)
-
+        cd[pl.ds(k_base, K_LOC), :] = c_solve(near)
+
+    c_far(SWEEPS - 1)
     a_rows = a_ref[pl.ds(pl.multiple_of(tube * RANK, RANK), RANK), :]
     a_out[...] = jnp.where(col == 0, a_rows[:, :RANK], a_rows[:, RANK:])
-    b_out[...] = bo_ref[tube][:, :RANK]
+    b_out[...] = bo_ref[tube].T[:RANK]
     c_out[...] = cd[:, :RANK]
+
+
+def emit(a_in, b_in, c_in, a_hbm, b_hbm, c_hbm, sems):
+    pairs = ((b_in, b_hbm), (a_in, a_hbm), (c_in, c_hbm))
+    copies = [pltpu.make_async_copy(src, dst, sems.at[n]) for n, (src, dst) in enumerate(pairs)]
+    for cp in copies:
+        cp.start()
+    for cp in copies:
+        cp.wait()
 
 
 def solution(mesh):
     def local(x_blk, b_own, c_full, ridge_lam):
+        shapes = ((64, RANK), (RANK, 256), (32, RANK))
+        x_blk, b_turn, c_full = (pltpu.with_memory_space_constraint(v, pltpu.HBM) for v in (x_blk, b_own.T, c_full))
         dma = pltpu.SemaphoreType.DMA
         vm = pltpu.VMEM
-        return pl.pallas_call(
+        a_new, b_new, c_new = pl.pallas_call(
             kernel,
-            out_shape=(jax.ShapeDtypeStruct((64, RANK), F32), jax.ShapeDtypeStruct((256, RANK), F32),
-                       jax.ShapeDtypeStruct((32, RANK), F32)),
-            in_specs=[pl.BlockSpec(memory_space=pl.ANY), pl.BlockSpec(memory_space=pltpu.VMEM),
-                      pl.BlockSpec(memory_space=pltpu.VMEM), pl.BlockSpec(memory_space=pltpu.SMEM)],
+            out_shape=tuple(pltpu.VMEM(shape, F32) for shape in shapes),
+            in_specs=[pl.BlockSpec(memory_space=pltpu.HBM), pl.BlockSpec(memory_space=pltpu.HBM),
+                      pl.BlockSpec(memory_space=pltpu.HBM), pl.BlockSpec(memory_space=pltpu.SMEM)],
             out_specs=(pl.BlockSpec(memory_space=pltpu.VMEM),) * 3,
             scratch_shapes=[
-                vm((K_LOC, I_LOC, J_TILE * J_TILES), F32),
+                vm((RANK, 256), F32),
+                vm((2 * K_LOC, RANK), F32),
+                vm((J_TILES, K_LOC, I_LOC, J_TILE), F32),
                 vm((J_TILES, K_LOC, I_LOC, J_TILE), BF16),
                 vm((K_LOC, I_HALF, LANES), F32),
                 vm((SWEEPS + 1, J_TILES, J_TILE, LANES), BF16),
@@ -298,24 +370,37 @@
                 vm((2, RANK, J_TILE), F32),
                 vm((SWEEPS, 2, RANK, J_TILE), F32),
                 vm((2, J_TILE, LANES), F32),
-                vm((SWEEPS + 1, RANK, LANES), F32),
-                vm((SWEEPS + 1, RANK, LANES), F32),
+                vm((RANK // 2, LANES), F32),
+                vm((7, RANK // 2, LANES), F32),
+                vm((RANK // 2, LANES), F32),
+                vm((SWEEPS, 3, RANK // 2, LANES), F32),
                 vm((RANK, LANES), F32),
                 vm((K_LOC, LANES), F32),
-                vm((SWEEPS, 7, K_LOC, LANES), F32),
-                vm((2 * K_LOC, LANES), F32),
-                dma((K_LOC,)), dma((3,)), dma((3,)),
+                vm((K_LOC // 2, LANES), F32),
+                vm((SWEEPS, 7, K_LOC // 2, LANES), F32),
+                vm((LANES, LANES), F32),
+                dma((2,)), dma((J_TILES, K_LOC // LOAD_K)), dma((3,)), dma((3,)),
                 dma((3, A_CHUNKS)), dma((SWEEPS, 3, A_CHUNKS)),
                 dma, dma((SWEEPS,)),
                 dma((2,)), dma((SWEEPS, 2)), dma((2,)), dma((SWEEPS, 2)),
                 dma((2,)), dma((SWEEPS, 2)),
-                dma((SWEEPS + 1,)), dma((SWEEPS + 1,)),
+                dma((7,)), dma((7,)), dma((3,)), dma((SWEEPS, 3)),
                 dma((7,)), dma((SWEEPS, 7)),
             ],
             compiler_params=pltpu.CompilerParams(collective_id=0, has_side_effects=True,
-                                                 vmem_limit_bytes=60 * 1024 * 1024),
+                                                 vmem_limit_bytes=52 * 1024 * 1024),
             name="als_sweeps",
-        )(x_blk, b_own, c_full, ridge_lam.reshape(1, 1))
+        )(x_blk, b_turn, c_full, ridge_lam.reshape(1, 1))
+        a_new, b_new, c_new = pl.pallas_call(
+            emit,
+            out_shape=tuple(jax.ShapeDtypeStruct(shape, F32) for shape in shapes),
+            in_specs=[pl.BlockSpec(memory_space=pltpu.VMEM)] * 3,
+            out_specs=(pl.BlockSpec(memory_space=pl.ANY),) * 3,
+            scratch_shapes=[dma((3,))],
+            compiler_params=pltpu.CompilerParams(vmem_limit_bytes=1024 * 1024),
+            name="emit_factors",
+        )(a_new, b_new, c_new)
+        return a_new, b_new.T, c_new
 
     return jax.shard_map(
         local,

time: 65.4 us -> 49.2 us (0.75)
  Pallas kernels: 57.9 us -> 47.6 us
  local copies, waits for them, and re-layouts: 5.9 us -> 0 us
    pallas_call x1 -> x2, Pallas kernels: 57.9 us -> 47.6 us  [the longest x1 46.9 us: local(): pl.pallas_call(kernel, out_shape=tuple((pltpu.VMEM(shape, F32) for shape...]
    unnamed x3 -> x0, local copies, waits for them, and re-layouts: 4.29 us -> none
    pallas_call x1 -> x0, local copies, waits for them, and re-layouts: 1.62 us -> none  [local(): pl.pallas_call(kernel, out_shape=(jax.ShapeDtypeStruct((64, RANK), F32),...]
where the time goes in v2:
time: 49.2 us; the launch traced here: 49 us
  Pallas kernels  47.6 us (97%)
  between operations  1.45 us (3%)
    pallas_call x1, Pallas kernels, local(): pl.pallas_call(kernel, out_shape=tuple((pltpu.VMEM(shape, F32) for shape...  46.9 us

profile of v2, /device:TPU:0, one launch (start us, length us, event | category | flops | bytes accessed | tf_op | source)
XLA Modules:
  0.0 49.0 jit_solution(2281343649743729210)
XLA Ops:
  1.3 46.9 %als_sweeps.1 = (f32[64,64]{1,0:T(8,128)S(1)}, f32[64,256]{1,0:T(8,128)S(1)}, f32[32,64]{1,0:T(8,128)S(1)}) custom-call(f32[16,256,1024]{2,1,0:T(8,128)} %x_hbm.1, f32[64,256]{1,0:T(8,128)} %bitcast.4, f32[32,64]{1,0:T(8,128)} %c_hbm.1, f32[1,1]{1,0:T(1,128)} %bitcast.3.lam_ref), custom_call_target="tpu_custom_call" | custom-call | tf_op jit(solution)/shard_map/als_sweeps/pallas_call | solution.py:345
  48.2 0.7 %emit_factors.1 = (f32[64,64]{1,0:T(8,128)}, f32[64,256]{1,0:T(8,128)}, f32[32,64]{1,0:T(8,128)}) custom-call(f32[64,64]{1,0:T(8,128)S(1)} %get-tuple-element.9.a_in, f32[64,256]{1,0:T(8,128)S(1)} %get-tuple-element.10.b_in, f32[32,64]{1,0:T(8,128)S(1)} %get-tuple-element.11.c_in), custom_call_target="tpu_custom_call" | custom-call | tf_op jit(solution)/shard_map/emit_factors/pallas_call | solution.py:394

commit v3 on v2

--- a/solution.py
+++ b/solution.py
@@ -15,7 +15,7 @@
 J_TILE = 256
 J_TILES = 4
 I_HALF = I_LOC // 2
-A_CHUNKS = 4
+A_CHUNKS = 2
 A_CHUNK = I_HALF // A_CHUNKS
 BLK = 16
 LOAD_K = 4
@@ -37,7 +37,7 @@
     return lax.dot_general(a, b, (((0,), (0,)), ((), ())), precision=precision, preferred_element_type=F32)
 
 
-def inverse_quad(gram_dup, lam):
+def inverse_quad(gram_dup, lam, between=None):
     row_ids = lax.broadcasted_iota(jnp.int32, (RANK, LANES), 0)
     lane_ids = lax.broadcasted_iota(jnp.int32, (RANK, LANES), 1)
     left_eye = jnp.where(lane_ids == row_ids, 1.0, 0.0).astype(F32)
@@ -69,6 +69,8 @@
             for c in range(BLK):
                 upd = upd - mults[t - b - 1][c] * jnp.broadcast_to(piv[c:c + 1, :], (BLK, LANES))
             blocks[t] = upd
+        if between is not None:
+            between(b)
     chol = jnp.concatenate(done, axis=0)
     inv_dup = jnp.where(lane_ids < RANK, pltpu.roll(chol, RANK, 1), chol)
     return dot_tn(inv_dup, inv_dup, HIGH)
@@ -76,7 +78,7 @@
 
 def kernel(x_hbm, b_hbm, c_hbm, lam_ref, a_out, b_out, c_out,
            b_init, c_init, xf, x4, u_ref, bd, bpk, brcv, cd, cb, a_ref, at_ref,
-           ma_snd, ma_rcv, ga_snd, ga_rcv, mb_snd, mb_d2d, mb_sum, mb_rcv, bo_ref,
+           ma_snd, ma_rcv, ga_snd, ga_rcv, mb_part, mb_d2d, mb_sum, mb_rcv, bo_ref,
            g0_snd, g0_rcv, gb_snd, gb_rcv, gb_all, mc_full, mc_snd, mc_rcv, inv_ref,
            in_sem, x_sem, b_ss, b_rs, ma_ss, ma_rs, ga_ss, ga_rs, md_ss, md_rs, my_ss, my_rs,
            ag_ss, ag_rs, g0_ss, g0_rs, gb_ss, gb_rs, mc_ss, mc_rs):
@@ -98,40 +100,52 @@
                                      xf.at[n, rows], x_sem.at[n, g])
 
     def tile_of(n):
-        r = 1 - row if n & 1 else row
-        t = 1 - tube if n & 2 else tube
-        return r * 2 + t
-
-    small = [pltpu.make_async_copy(b_hbm, b_init, in_sem.at[0]), pltpu.make_async_copy(c_hbm, c_init, in_sem.at[1])]
+        if n == 0:
+            return row * 2 + tube
+        if n == 1:
+            return (1 - row) * 2 + tube
+        return (3 - n) * 2 + 1 - tube
+
+    small = [pltpu.make_async_copy(src, dst, in_sem.at[n])
+             for n, (src, dst) in enumerate(((b_hbm, b_init), (c_hbm, c_init)))]
     for cp in small:
         cp.start()
 
     def load_start(n):
         for g in range(K_LOC // LOAD_K):
-            load(n, g).start()
+            load(n, g).start(priority=1)
 
     load_start(0)
+    load_start(1)
     barrier = pltpu.get_barrier_semaphore()
     for d in range(1, 8):
         pl.semaphore_signal(barrier, inc=1, device_id=peer(d), device_id_type=MESH)
 
-    lam = lam_ref[0, 0]
     lanes_b = lax.broadcasted_iota(jnp.int32, (I_HALF, LANES), 1)
     low_half = lanes_b < RANK
     for cp in small:
         cp.wait()
-    for n in range(1, J_TILES):
+    for n in range(2, J_TILES):
         load_start(n)
+    lam = lam_ref[0, 0]
     b_turn = b_init[...]
     bpk[...] = jnp.concatenate([b_turn[:, :I_HALF], b_turn[:, I_HALF:]], axis=0).T.astype(BF16)
     cd[...] = jnp.concatenate([c_init[...], c_init[...]], axis=1)
     pl.semaphore_wait(barrier, 7)
 
-    def b_send(n):
-        return send(bpk, brcv.at[n - 1], b_ss.at[n - 1], b_rs.at[n - 1], (n & 1) | (n & 2) << 1)
-
-    for n in (3, 2, 1):
-        b_send(n).start()
+    def b_send(src, n, d, ss):
+        return send(src, brcv.at[n - 1], b_ss.at[ss], b_rs.at[n - 1], d)
+
+    @pl.when(row == 0)
+    def _():
+        b_send(bpk, 3, 4, 1).start()
+        b_send(bpk, 3, 5, 2).start()
+
+    @pl.when(row == 1)
+    def _():
+        b_send(bpk, 2, 4, 1).start()
+
+    b_send(bpk, 1, 1, 0).start()
 
     def unpack_b(packed, n):
         wide = packed.astype(F32)
@@ -158,7 +172,7 @@
 
     def gram_b_start(s):
         gb_snd[...] = gram_pack([bd[s + 1, row * 2], bd[s + 1, row * 2 + 1]])
-        for d in (3, 2, 1):
+        for d in (2, 3, 1):
             gb_send(s, d).start()
 
     def gram_b_finish(s):
@@ -166,11 +180,15 @@
             gb_send(s, d).wait()
         gb_all[...] = gram_unpack((gb_snd[...] + gb_rcv[s, 0]) + (gb_rcv[s, 1] + gb_rcv[s, 2]))
 
+    low_chunk = lax.broadcasted_iota(jnp.int32, (A_CHUNK, LANES), 1) < RANK
+
     def pack_u(u_both):
-        return jnp.where(low_half, u_both[:I_HALF], u_both[I_HALF:])
-
-    def u_pass(slot, tiles, first, last, staged=None):
-        for k in range(K_LOC):
+        quarters = [u_both[n * A_CHUNK:(n + 1) * A_CHUNK] for n in range(2 * A_CHUNKS)]
+        return jnp.concatenate([jnp.where(low_chunk, quarters[2 * c], quarters[2 * c + 1])
+                                for c in range(A_CHUNKS)], axis=0)
+
+    def u_pass(slot, tiles, first, last, staged=None, slabs=range(K_LOC)):
+        for k in slabs:
             u_both = jnp.zeros((I_LOC, LANES), F32)
             for jt in tiles:
                 if staged is None:
@@ -192,11 +210,19 @@
         g0_send(d).start()
     for n in range(J_TILES):
         if n > 0:
-            b_send(n).wait()
+            b_send(bpk, n, 1, 0).wait_recv()
+            if n == 2:
+                @pl.when(row == 1)
+                def _():
+                    b_send(brcv.at[1], 2, 1, 2).start()
             unpack_b(brcv[n - 1], n)
-        for g in range(K_LOC // LOAD_K):
-            load(n, g).wait()
-        u_pass(0, [tile_of(n)], n == 0, False, staged=n)
+        step = K_LOC // 2 if n == J_TILES - 1 else K_LOC
+        for k in range(0, K_LOC, step):
+            for g in range(k // LOAD_K, (k + step) // LOAD_K):
+                load(n, g).wait()
+            u_pass(0, [tile_of(n)], n == 0, False, staged=n, slabs=range(k, k + step))
+    for ss in range(3):
+        b_send(bpk, 1, 1, ss).wait_send()
     for d in range(1, 8):
         g0_send(d).wait()
     here = (g0_snd[...] + g0_rcv[0]) + (g0_rcv[3] + g0_rcv[4])
@@ -223,17 +249,19 @@
     @pl.loop(0, SWEEPS)
     def _(s):
         c_own = cd[pl.ds(k_base, K_LOC), :]
-        a_copies = []
+        def a_send(ch, d):
+            rows = pl.ds(ch * A_CHUNK, A_CHUNK)
+            n = d // 2 - 1
+            return send(ma_snd.at[rows], ma_rcv.at[s, n, rows], ma_ss.at[n, ch], ma_rs.at[s, n, ch], d)
+
         for ch in range(A_CHUNKS):
-            rows = pl.ds(ch * A_CHUNK, A_CHUNK)
             part = jnp.zeros((A_CHUNK, LANES), F32)
             for k in range(K_LOC):
                 part = part + u_ref[k, ch * A_CHUNK:(ch + 1) * A_CHUNK, :] * c_own[k:k + 1, :]
             ma_snd[ch * A_CHUNK:(ch + 1) * A_CHUNK, :] = part
-            for n, d in ((2, 6), (1, 4), (0, 2)):
-                cp = send(ma_snd.at[rows], ma_rcv.at[s, n, rows], ma_ss.at[n, ch], ma_rs.at[s, n, ch], d)
-                cp.start()
-                a_copies.append(cp)
+            for d in (6, 4, 2):
+                a_send(ch, d).start()
+
         @pl.when(s > 0)
         def _():
             c_far(s - 1)
@@ -247,49 +275,78 @@
         quad_r = lax.broadcasted_iota(jnp.int32, (LANES, LANES), 0) < RANK
         quad_c = lax.broadcasted_iota(jnp.int32, (LANES, LANES), 1) < RANK
         inv_diag = jnp.where(quad_r == quad_c, inv_a, 0.0)
-        for cp in a_copies:
-            cp.wait()
-        mtt_a = (ma_snd[...] + ma_rcv[s, 0]) + (ma_rcv[s, 1] + ma_rcv[s, 2])
-        a_new = dot_nn(mtt_a, inv_diag, HIGH)
-        a_ref[...] = a_new
-        a_turn = a_new.T.astype(BF16)
-        at_ref[:, :I_HALF] = a_turn[:RANK]
-        at_ref[:, I_HALF:] = a_turn[RANK:]
-
-        def v_tile(jt):
+
+        def a_solve(ch):
+            rows = slice(ch * A_CHUNK, (ch + 1) * A_CHUNK)
+            for d in (2, 4, 6):
+                a_send(ch, d).wait()
+            mtt_a = (ma_snd[rows, :] + ma_rcv[s, 0, rows, :]) + (ma_rcv[s, 1, rows, :] + ma_rcv[s, 2, rows, :])
+            a_new = dot_nn(mtt_a, inv_diag, HIGH)
+            a_ref[rows, :] = a_new
+            a_turn = a_new.T
+            at_ref[ch] = jnp.concatenate([a_turn[:RANK], a_turn[RANK:]], axis=1).astype(BF16)
+
+        def v_tile(jt, ch):
             acc = jnp.zeros((RANK, J_TILE), F32)
             for k in range(K_LOC):
-                v_kt = dot_nn(at_ref[...], x4[jt, k])
+                v_kt = dot_nn(at_ref[ch], x4[jt, k, ch * I_HALF:(ch + 1) * I_HALF, :])
                 c_col = cb[k]
                 acc = acc + v_kt * jnp.concatenate([c_col, c_col], axis=1)
             return acc
 
-        d_copies = []
-        for q in range(2):
-            mb_snd[q] = v_tile((1 - row) * 2 + q)
-            cp = send(mb_snd.at[q], mb_d2d.at[s, q], md_ss.at[q], md_rs.at[s, q], 1)
-            cp.start()
-            d_copies.append(cp)
-            if q == 0:
-                at = at_ref[...]
-                ga_snd[...] = dot_nt(at, jnp.concatenate([at, at], axis=0))
-                ga_cp = send(ga_snd, ga_rcv.at[s], ga_ss, ga_rs.at[s], 1)
-                ga_cp.start()
-        y_copies = []
-        for q in range(2):
-            own = v_tile(row * 2 + q)
-            d_copies[q].wait()
-            mb_sum[q] = own + mb_d2d[s, q]
-            cp = send(mb_sum.at[q], mb_rcv.at[s, q], my_ss.at[q], my_rs.at[s, q], 4)
-            cp.start()
-            y_copies.append(cp)
-        ga_cp.wait()
+        def d_send(q):
+            return send(mb_part.at[(1 - row) * 2 + q], mb_d2d.at[s, q], md_ss.at[q], md_rs.at[s, q], 1)
+
+        def y_send(q):
+            return send(mb_sum.at[q], mb_rcv.at[s, q], my_ss.at[q], my_rs.at[s, q], 4)
+
+        def ga_send():
+            return send(ga_snd, ga_rcv.at[s], ga_ss, ga_rs.at[s], 1)
+
+        def reduce_cores(q):
+            d_send(q).wait_recv()
+            mb_sum[q] = mb_part[row * 2 + q] + mb_d2d[s, q]
+            y_send(q).start()
+
+        a_solve(0)
+        for jt in range(J_TILES):
+            mb_part[jt] = v_tile(jt, 0)
+        a_solve(1)
+        for n, jt in enumerate((0, 2, 1, 3)):
+            mb_part[jt] = mb_part[jt] + v_tile(jt, 1)
+            if n == 1:
+                ga_snd[...] = sum(dot_nt(at_ref[ch], jnp.concatenate([at_ref[ch], at_ref[ch]], axis=0))
+                                  for ch in range(A_CHUNKS))
+
+            @pl.when(row != jt // 2)
+            def _():
+                d_send(jt % 2).start()
+
+            if n % 2 == 0:
+                @pl.when(row == 0)
+                def _():
+                    reduce_cores(n // 2)
+            if n == 1:
+                ga_send().start()
+
+        def late_reduce(b):
+            if b == 1:
+                @pl.when(row == 1)
+                def _():
+                    reduce_cores(1)
+
+        @pl.when(row == 1)
+        def _():
+            reduce_cores(0)
+
+        ga_send().wait()
         gram_a = ga_snd[...] + ga_rcv[s]
-        inv_b = inverse_quad(gram_a * gram_c, lam)
+        inv_b = inverse_quad(gram_a * gram_c, lam, late_reduce)
         g_copies = []
 
         def b_solve(q):
-            y_copies[q].wait()
+            y_send(q).wait()
+            d_send(q).wait_send()
             b_new = dot_tn(mb_sum[q] + mb_rcv[s, q], inv_b[:RANK], HIGH)
             bo_ref[q] = b_new
             tile = bd.at[s + 1, row * 2 + q]
@@ -299,19 +356,18 @@
             g_copies.append(cp)
 
         b_solve(0)
-        u_pass(s + 1, [row * 2], True, False)
         b_solve(1)
         gram_b_start(s)
-        g_copies[0].wait()
-        u_pass(s + 1, [row * 2 + 1, (1 - row) * 2], False, False)
-        g_copies[1].wait()
-        u_pass(s + 1, [(1 - row) * 2 + 1], False, True)
+        u_pass(s + 1, [row * 2, row * 2 + 1], True, False)
+        for cp in g_copies:
+            cp.wait()
+        u_pass(s + 1, [(1 - row) * 2, (1 - row) * 2 + 1], False, True)
 
         part_c = mc_full[...]
         part_c = part_c + pltpu.roll(part_c, RANK, 1)
         low_c = lax.broadcasted_iota(jnp.int32, (K_LOC // 2, LANES), 1) < RANK
         mc_snd[...] = jnp.where(low_c, part_c[:K_LOC // 2], part_c[K_LOC // 2:])
-        for d in (2, 3, 1, 6, 7, 4, 5):
+        for d in (6, 7, 2, 3, 4, 5, 1):
             c_send(s, d).start()
         gram_b_finish(s)
         inv_ref[...] = inverse_quad(gram_a * gb_all[...], lam)
@@ -321,8 +377,8 @@
         cd[pl.ds(k_base, K_LOC), :] = c_solve(near)
 
     c_far(SWEEPS - 1)
-    a_rows = a_ref[pl.ds(pl.multiple_of(tube * RANK, RANK), RANK), :]
-    a_out[...] = jnp.where(col == 0, a_rows[:, :RANK], a_rows[:, RANK:])
+    a_rows = a_ref[pl.ds(pl.multiple_of(col * A_CHUNK, A_CHUNK), A_CHUNK), :]
+    a_out[...] = jnp.where(tube == 0, a_rows[:, :RANK], a_rows[:, RANK:])
     b_out[...] = bo_ref[tube].T[:RANK]
     c_out[...] = cd[:, :RANK]
 
@@ -339,14 +395,14 @@
 def solution(mesh):
     def local(x_blk, b_own, c_full, ridge_lam):
         shapes = ((64, RANK), (RANK, 256), (32, RANK))
-        x_blk, b_turn, c_full = (pltpu.with_memory_space_constraint(v, pltpu.HBM) for v in (x_blk, b_own.T, c_full))
+        operands = (x_blk, b_own.T, c_full)
+        operands = [pltpu.with_memory_space_constraint(v, pltpu.HBM) for v in operands]
         dma = pltpu.SemaphoreType.DMA
         vm = pltpu.VMEM
         a_new, b_new, c_new = pl.pallas_call(
             kernel,
             out_shape=tuple(pltpu.VMEM(shape, F32) for shape in shapes),
-            in_specs=[pl.BlockSpec(memory_space=pltpu.HBM), pl.BlockSpec(memory_space=pltpu.HBM),
-                      pl.BlockSpec(memory_space=pltpu.HBM), pl.BlockSpec(memory_space=pltpu.SMEM)],
+            in_specs=[pl.BlockSpec(memory_space=pltpu.HBM)] * 3 + [pl.BlockSpec(memory_space=pltpu.SMEM)],
             out_specs=(pl.BlockSpec(memory_space=pltpu.VMEM),) * 3,
             scratch_shapes=[
                 vm((RANK, 256), F32),
@@ -360,12 +416,12 @@
                 vm((2 * K_LOC, LANES), F32),
                 vm((K_LOC, RANK, LANES), F32),
                 vm((I_HALF, LANES), F32),
-                vm((RANK, I_LOC), BF16),
+                vm((A_CHUNKS, RANK, I_HALF), BF16),
                 vm((I_HALF, LANES), F32),
                 vm((SWEEPS, 3, I_HALF, LANES), F32),
                 vm((RANK, LANES), F32),
                 vm((SWEEPS, RANK, LANES), F32),
-                vm((2, RANK, J_TILE), F32),
+                vm((J_TILES, RANK, J_TILE), F32),
                 vm((SWEEPS, 2, RANK, J_TILE), F32),
                 vm((2, RANK, J_TILE), F32),
                 vm((SWEEPS, 2, RANK, J_TILE), F32),
@@ -390,7 +446,7 @@
             compiler_params=pltpu.CompilerParams(collective_id=0, has_side_effects=True,
                                                  vmem_limit_bytes=52 * 1024 * 1024),
             name="als_sweeps",
-        )(x_blk, b_turn, c_full, ridge_lam.reshape(1, 1))
+        )(*operands, ridge_lam.reshape(1, 1))
         a_new, b_new, c_new = pl.pallas_call(
             emit,
             out_shape=tuple(jax.ShapeDtypeStruct(shape, F32) for shape in shapes),

time: 49.2 us -> 46.2 us (0.939)
  Pallas kernels: 47.6 us -> 44.7 us
    pallas_call x1, Pallas kernels: 46.9 us -> 44 us  [local(): pl.pallas_call(kernel, out_shape=tuple((pltpu.VMEM(shape, F32) for shape...]
where the time goes in v3:
time: 46.2 us; the launch traced here: 46.1 us
  Pallas kernels  44.7 us (97%)
  between operations  1.45 us (3%)
    pallas_call x1, Pallas kernels, local(): pl.pallas_call(kernel, out_shape=tuple((pltpu.VMEM(shape, F32) for shape...  44 us

profile of v3, /device:TPU:0, one launch (start us, length us, event | category | flops | bytes accessed | tf_op | source)
XLA Modules:
  0.0 46.1 jit_solution(17642355798866476243)
XLA Ops:
  1.3 44.0 %als_sweeps.1 = (f32[64,64]{1,0:T(8,128)S(1)}, f32[64,256]{1,0:T(8,128)S(1)}, f32[32,64]{1,0:T(8,128)S(1)}) custom-call(f32[16,256,1024]{2,1,0:T(8,128)} %x_hbm.1, f32[64,256]{1,0:T(8,128)} %bitcast.4, f32[32,64]{1,0:T(8,128)} %c_hbm.1, f32[1,1]{1,0:T(1,128)} %bitcast.3.lam_ref), custom_call_target="tpu_custom_call" | custom-call | tf_op jit(solution)/shard_map/als_sweeps/pallas_call | solution.py:402
  45.3 0.7 %emit_factors.1 = (f32[64,64]{1,0:T(8,128)}, f32[64,256]{1,0:T(8,128)}, f32[32,64]{1,0:T(8,128)}) custom-call(f32[64,64]{1,0:T(8,128)S(1)} %get-tuple-element.9.a_in, f32[64,256]{1,0:T(8,128)S(1)} %get-tuple-element.10.b_in, f32[32,64]{1,0:T(8,128)S(1)} %get-tuple-element.11.c_in), custom_call_target="tpu_custom_call" | custom-call | tf_op jit(solution)/shard_map/emit_factors/pallas_call | solution.py:450

commit v4 on v3

v4 whole, which is shorter than its diff:
```python
import functools

import jax
import jax.numpy as jnp
from jax import lax
from jax.experimental import pallas as pl
from jax.experimental.pallas import tpu as pltpu
from jax.sharding import PartitionSpec as P

SWEEPS = 2
RANK = 64
LANES = 128
K_LOC = 16
I_LOC = 256
J_TILE = 256
J_TILES = 4
I_HALF = I_LOC // 2
A_CHUNKS = 2
BLK = 16
LOAD_K = 4
MESH = pl.DeviceIdType.MESH
HIGH = lax.Precision.HIGHEST
F32 = jnp.float32
BF16 = jnp.bfloat16


def dot_nn(a, b, precision=None):
    return lax.dot_general(a, b, (((1,), (0,)), ((), ())), precision=precision, preferred_element_type=F32)


def dot_nt(a, b, precision=None):
    return lax.dot_general(a, b, (((1,), (1,)), ((), ())), precision=precision, preferred_element_type=F32)


def dot_tn(a, b, precision=None):
    return lax.dot_general(a, b, (((0,), (0,)), ((), ())), precision=precision, preferred_element_type=F32)


def spd_inverse(gram_dup, lam, between=None):
    row_ids = lax.broadcasted_iota(jnp.int32, (RANK, LANES), 0)
    lane_ids = lax.broadcasted_iota(jnp.int32, (RANK, LANES), 1)
    left_eye = jnp.where(lane_ids == row_ids, 1.0, 0.0).astype(F32)
    right_eye = jnp.where(lane_ids == row_ids + RANK, 1.0, 0.0).astype(F32)
    aug = jnp.where(lane_ids < RANK, left_eye, gram_dup + lam * right_eye)
    n_blk = RANK // BLK
    blocks = [aug[b * BLK:(b + 1) * BLK] for b in range(n_blk)]
    sub_ids = lax.broadcasted_iota(jnp.int32, (BLK, LANES), 0)

    def lane(block, b, c):
        at = RANK + b * BLK + c
        return jnp.broadcast_to(block[:, at:at + 1], (BLK, LANES))

    def sublane(block, c):
        return jnp.broadcast_to(block[c:c + 1, :], (BLK, LANES))

    done = []
    for b in range(n_blk):
        piv = blocks[b]
        cols = [lane(piv, b, c) for c in range(BLK)]
        mults = [[lane(blocks[t], b, c) for c in range(BLK)] for t in range(b + 1, n_blk)]
        chol_rows = jnp.zeros((BLK, LANES), F32)
        diag = sublane(cols[0], 0)
        for c in range(BLK):
            is_row = sub_ids == c
            root = lax.rsqrt(diag)
            elts = {c2: sublane(cols[c2], c) * root for c2 in range(c + 1, BLK)}
            if c + 1 < BLK:
                diag = sublane(cols[c + 1], c + 1) - (sublane(cols[c], c + 1) * root) * elts[c + 1]
            scaled_col = cols[c] * root
            scaled_row = sublane(piv, c) * root
            chol_rows = jnp.where(is_row, scaled_row, chol_rows)
            piv = jnp.where(is_row, scaled_row * root, piv - scaled_col * scaled_row)
            for c2 in range(c + 1, BLK):
                cols[c2] = jnp.where(is_row, elts[c2] * root, cols[c2] - scaled_col * elts[c2])
        done.append(chol_rows)
        for t in range(b + 1, n_blk):
            upd = blocks[t]
            for c in range(BLK):
                upd = upd - mults[t - b - 1][c] * sublane(piv, c)
            blocks[t] = upd
        if between is not None:
            between(b)
    low_inv = jnp.concatenate(done, axis=0)[:, :RANK]
    return dot_tn(low_inv, low_inv, HIGH)


def kernel(x_hbm, b_hbm, c_hbm, lam_ref, a_out, b_out, c_out,
           b_init, c_init, xf, x4, x4t, u_ref, bt, c_own, c_other, cb, a32_ref, at_ref,
           ma_snd, ma_rcv, ga_snd, ga_rcv, mb_part, mb_d2d, mb_sum, mb_rcv, bo_ref,
           g0_snd, g0_rcv, gb_snd, gb_rcv, gb_all, mc_snd, mc_rcv, inv_ref,
           in_sem, x_sem, b_ss, b_rs, ma_ss, ma_rs, ga_ss, ga_rs, md_ss, md_rs, my_ss, my_rs,
           ag_ss, ag_rs, g0_ss, g0_rs, gb_ss, gb_rs, mc_ss, mc_rs):
    tube, col, row = lax.axis_index("tube"), lax.axis_index("col"), lax.axis_index("row")

    def peer(d):
        t = 1 - tube if d & 4 else tube
        c = 1 - col if d & 2 else col
        r = 1 - row if d & 1 else row
        return (t, c, r)

    def send(src, dst, ss, rs, d):
        return pltpu.make_async_remote_copy(src_ref=src, dst_ref=dst, send_sem=ss, recv_sem=rs,
                                            device_id=peer(d), device_id_type=MESH)

    def load(n, g):
        rows = pl.ds(g * LOAD_K, LOAD_K)
        return pltpu.make_async_copy(x_hbm.at[rows, :, pl.ds(pl.multiple_of(tile_of(n) * J_TILE, J_TILE), J_TILE)],
                                     xf.at[n, rows], x_sem.at[n, g])

    def tile_of(n):
        if n == 0:
            return row * 2 + tube
        if n == 1:
            return (1 - row) * 2 + tube
        return (3 - n) * 2 + 1 - tube

    small = [pltpu.make_async_copy(src, dst, in_sem.at[n])
             for n, (src, dst) in enumerate(((b_hbm, b_init), (c_hbm, c_init)))]
    for cp in small:
        cp.start()

    def load_start(n):
        for g in range(K_LOC // LOAD_K):
            load(n, g).start(priority=1)

    load_start(0)
    load_start(1)
    barrier = pltpu.get_barrier_semaphore()
    for d in range(1, 8):
        pl.semaphore_signal(barrier, inc=1, device_id=peer(d), device_id_type=MESH)

    k_base = pl.multiple_of(tube * K_LOC, K_LOC)
    k_far = pl.multiple_of((1 - tube) * K_LOC, K_LOC)
    lam = lam_ref[0, 0]
    for cp in small:
        cp.wait()
    for n in range(2, J_TILES):
        load_start(n)
    bt[0, row * 2 + tube] = b_init[...].astype(BF16)

    def turn_c(rows):
        wide = jnp.concatenate([rows, jnp.zeros((K_LOC, RANK), F32)], axis=1)
        return jnp.concatenate([wide, jnp.zeros((LANES - K_LOC, LANES), F32)], axis=0).T[:RANK]

    def spread_c():
        for k in range(K_LOC):
            cb[k] = jnp.broadcast_to(c_own[:, k:k + 1], (RANK, LANES))

    c_own[...] = turn_c(c_init[pl.ds(k_base, K_LOC), :])
    c_other[...] = turn_c(c_init[pl.ds(k_far, K_LOC), :])
    pl.semaphore_wait(barrier, 7)

    def b_send(tile, n, d, ss):
        return send(bt.at[0, tile], bt.at[0, tile], b_ss.at[ss], b_rs.at[n - 1], d)

    own_tile = row * 2 + tube

    @pl.when(row == 0)
    def _():
        b_send(own_tile, 3, 4, 1).start()
        b_send(own_tile, 3, 5, 2).start()

    @pl.when(row == 1)
    def _():
        b_send(own_tile, 2, 4, 1).start()

    b_send(own_tile, 1, 1, 0).start()

    half_lanes = lax.broadcasted_iota(jnp.int32, (RANK // 2, LANES), 1) < RANK

    def gram_dup(turned):
        return dot_nt(turned, jnp.concatenate([turned, turned], axis=0))

    def gram_pack(tiles):
        gram = sum(gram_dup(tile) for tile in tiles)
        return jnp.where(half_lanes, gram[:RANK // 2], gram[RANK // 2:])

    def gram_unpack(packed):
        turned = pltpu.roll(packed, RANK, 1)
        return jnp.concatenate([jnp.where(half_lanes, packed, turned), jnp.where(half_lanes, turned, packed)], axis=0)

    def g0_send(d):
        return send(g0_snd, g0_rcv.at[d - 1], g0_ss.at[d - 1], g0_rs.at[d - 1], d)

    def gb_send(s, d):
        return send(gb_snd, gb_rcv.at[s, d - 1], gb_ss.at[d - 1], gb_rs.at[s, d - 1], d)

    def gram_b_start(s):
        gb_snd[...] = gram_pack([bt[s + 1, row * 2], bt[s + 1, row * 2 + 1]])
        for d in (2, 3, 1):
            gb_send(s, d).start()

    def gram_b_finish(s):
        for d in (3, 2, 1):
            gb_send(s, d).wait_recv()
        gb_all[...] = gram_unpack((gb_snd[...] + gb_rcv[s, 0]) + (gb_rcv[s, 1] + gb_rcv[s, 2]))

    lanes_c = lax.broadcasted_iota(jnp.int32, (K_LOC // 2, LANES), 1)

    def u_pass(slot, tiles, first, last, staged=None, slabs=range(K_LOC)):
        packed = jnp.zeros((K_LOC // 2, LANES), F32)
        for k in slabs:
            u_new = jnp.zeros((RANK, I_LOC), F32)
            for jt in tiles:
                if staged is None:
                    x_turn = x4t[jt, k]
                else:
                    x_tile = xf[staged, k].astype(BF16)
                    x4[jt, k] = x_tile
                    x_turn = x_tile.T
                    x4t[jt, k] = x_turn
                u_new = u_new + dot_nn(bt[slot, jt], x_turn)
            if not first:
                u_new = u_ref[k] + u_new
            u_ref[k] = u_new
            if last:
                prod = u_new[:, :I_HALF] * a32_ref[0] + u_new[:, I_HALF:] * a32_ref[1]
                for g in range(RANK // 8):
                    total = jnp.sum(prod[8 * g:8 * g + 8], axis=1, keepdims=True)
                    packed = jnp.where(lanes_c == K_LOC * g + k, total, packed)
        return packed

    g0_snd[...] = gram_pack([bt[0, own_tile]])
    for d in (7, 6, 3, 2, 5, 4, 1):
        g0_send(d).start()
    spread_c()
    for n in range(J_TILES):
        if n > 0:
            b_send(tile_of(n), n, 1, 0).wait_recv()
            if n == 2:
                @pl.when(row == 1)
                def _():
                    b_send(tile_of(2), 2, 1, 2).start()
        step = K_LOC // 2 if n == J_TILES - 1 else K_LOC
        for k in range(0, K_LOC, step):
            for g in range(k // LOAD_K, (k + step) // LOAD_K):
                load(n, g).wait()
            u_pass(0, [tile_of(n)], n == 0, False, staged=n, slabs=range(k, k + step))
    for ss in range(3):
        b_send(own_tile, 1, 1, ss).wait_send()
    for d in range(1, 8):
        g0_send(d).wait()
    here = (g0_snd[...] + g0_rcv[0]) + (g0_rcv[3] + g0_rcv[4])
    there = (g0_rcv[1] + g0_rcv[2]) + (g0_rcv[5] + g0_rcv[6])
    gb_all[...] = gram_unpack(here + there)

    def c_send(s, d):
        return send(mc_snd, mc_rcv.at[s, d - 1], mc_ss.at[d - 1], mc_rs.at[s, d - 1], d)

    def c_solve(packed):
        turned = [packed if g == 0 else pltpu.roll(packed, LANES - K_LOC * g, 1) for g in range(RANK // 8)]
        turned = jnp.concatenate(turned, axis=0)
        lane = lax.broadcasted_iota(jnp.int32, (RANK, LANES), 1)
        return dot_nn(inv_ref[...], jnp.where(lane < K_LOC, turned, 0.0), HIGH)

    def c_sent(s):
        for d in range(1, 8):
            c_send(s, d).wait_send()

    def c_far(s):
        for d in (4, 5, 6, 7):
            c_send(s, d).wait_recv()
        far = (mc_rcv[s, 3] + mc_rcv[s, 4]) + (mc_rcv[s, 5] + mc_rcv[s, 6])
        c_other[...] = c_solve(far)

    @pl.loop(0, SWEEPS)
    def _(s):
        def a_send(ch, d):
            n = d // 2 - 1
            return send(ma_snd.at[ch], ma_rcv.at[s, n, ch], ma_ss.at[n, ch], ma_rs.at[s, n, ch], d)

        for ch in range(A_CHUNKS):
            part = jnp.zeros((RANK, I_HALF), F32)
            for k in range(K_LOC):
                part = part + u_ref[k, :, ch * I_HALF:(ch + 1) * I_HALF] * cb[k]
            ma_snd[ch] = part
            for d in (6, 4, 2):
                a_send(ch, d).start()

        @pl.when(s > 0)
        def _():
            c_far(s - 1)

        gram_c = gram_dup(c_own[...].astype(BF16)) + gram_dup(c_other[...].astype(BF16))
        inv_a = spd_inverse(gb_all[...] * gram_c, lam)
        def a_solve(ch):
            for d in (2, 4, 6):
                a_send(ch, d).wait_recv()
            mtt_a = (ma_snd[ch] + ma_rcv[s, 0, ch]) + (ma_rcv[s, 1, ch] + ma_rcv[s, 2, ch])
            a_turn = dot_nn(inv_a, mtt_a, HIGH)
            a32_ref[ch] = a_turn
            at_ref[ch] = a_turn.astype(BF16)

        def v_tile(jt, ch):
            acc = jnp.zeros((RANK, J_TILE), F32)
            for k in range(K_LOC):
                v_kt = dot_nn(at_ref[ch], x4[jt, k, ch * I_HALF:(ch + 1) * I_HALF, :])
                c_col = cb[k]
                acc = acc + v_kt * jnp.concatenate([c_col, c_col], axis=1)
            return acc

        def d_send(q):
            return send(mb_part.at[(1 - row) * 2 + q], mb_d2d.at[s, q], md_ss.at[q], md_rs.at[s, q], 1)

        def y_send(q):
            return send(mb_sum.at[q], mb_rcv.at[s, q], my_ss.at[q], my_rs.at[s, q], 4)

        def ga_send():
            return send(ga_snd, ga_rcv.at[s], ga_ss, ga_rs.at[s], 1)

        def reduce_cores(q):
            d_send(q).wait_recv()
            mb_sum[q] = mb_part[row * 2 + q] + mb_d2d[s, q]
            y_send(q).start()

        a_solve(0)
        for jt in range(J_TILES):
            mb_part[jt] = v_tile(jt, 0)
        a_solve(1)

        def v_last(jt):
            mb_part[jt] = mb_part[jt] + v_tile(jt, 1)

        v_last(0)

        @pl.when(row == 0)
        def _():
            reduce_cores(0)

        @pl.when(row == 1)
        def _():
            d_send(0).start()

        v_last(2)
        ga_snd[...] = sum(gram_dup(at_ref[ch]) for ch in range(A_CHUNKS))

        @pl.when(row == 0)
        def _():
            d_send(0).start()

        ga_send().start()
        v_last(1)
        v_last(3)

        @pl.when(row == 0)
        def _():
            reduce_cores(1)

        d_send(1).start()

        def late_reduce(b):
            if b == 0:
                @pl.when(row == 1)
                def _():
                    reduce_cores(1)

        @pl.when(row == 1)
        def _():
            reduce_cores(0)

        ga_send().wait_recv()
        gram_a = ga_snd[...] + ga_rcv[s]
        inv_b = spd_inverse(gram_a * gram_c, lam, late_reduce)
        g_copies = []

        def b_solve(q):
            y_send(q).wait_recv()
            b_new = dot_nn(inv_b, mb_sum[q] + mb_rcv[s, q], HIGH)
            bo_ref[q] = b_new
            tile = bt.at[s + 1, row * 2 + q]
            tile[...] = b_new.astype(BF16)
            cp = send(tile, tile, ag_ss.at[q], ag_rs.at[s, q], 1)
            cp.start()
            g_copies.append(cp)

        b_solve(0)
        b_solve(1)
        gram_b_start(s)
        u_pass(s + 1, [row * 2, row * 2 + 1], True, False)
        for cp in g_copies:
            cp.wait_recv()
        part_c = u_pass(s + 1, [(1 - row) * 2, (1 - row) * 2 + 1], False, True)

        @pl.when(s > 0)
        def _():
            c_sent(s - 1)

        mc_snd[...] = part_c
        for d in (6, 7, 2, 3, 4, 5, 1):
            c_send(s, d).start()
        gram_b_finish(s)
        inv_ref[...] = spd_inverse(gram_a * gb_all[...], lam)
        for ch in range(A_CHUNKS):
            for d in (2, 4, 6):
                a_send(ch, d).wait_send()
        ga_send().wait_send()
        for q in range(2):
            d_send(q).wait_send()
            y_send(q).wait_send()
            g_copies[q].wait_send()
        for d in (1, 2, 3):
            gb_send(s, d).wait_send()
        for d in (1, 2, 3):
            c_send(s, d).wait_recv()
        near = (mc_snd[...] + mc_rcv[s, 0]) + (mc_rcv[s, 1] + mc_rcv[s, 2])
        c_own[...] = c_solve(near)
        spread_c()

    c_far(SWEEPS - 1)
    c_sent(SWEEPS - 1)
    a_rows = a32_ref[col].T
    a_out[...] = jnp.where(tube == 0, a_rows[:I_HALF // 2], a_rows[I_HALF // 2:])
    b_out[...] = bo_ref[tube]
    c_out[pl.ds(k_base, K_LOC), :] = c_own[...].T[:K_LOC]
    c_out[pl.ds(k_far, K_LOC), :] = c_other[...].T[:K_LOC]


def emit(a_in, b_in, c_in, a_hbm, b_hbm, c_hbm, sems):
    pairs = ((b_in, b_hbm), (a_in, a_hbm), (c_in, c_hbm))
    copies = [pltpu.make_async_copy(src, dst, sems.at[n]) for n, (src, dst) in enumerate(pairs)]
    for cp in copies:
        cp.start()
    for cp in copies:
        cp.wait()


def solution(mesh):
    def local(x_blk, b_own, c_full, ridge_lam):
        shapes = ((64, RANK), (RANK, 256), (32, RANK))
        operands = (x_blk, b_own.T, c_full)
        operands = [pltpu.with_memory_space_constraint(v, pltpu.HBM) for v in operands]
        dma = pltpu.SemaphoreType.DMA
        vm = pltpu.VMEM
        a_new, b_new, c_new = pl.pallas_call(
            kernel,
            out_shape=tuple(pltpu.VMEM(shape, F32) for shape in shapes),
            in_specs=[pl.BlockSpec(memory_space=pltpu.HBM)] * 3 + [pl.BlockSpec(memory_space=pltpu.SMEM)],
            out_specs=(pl.BlockSpec(memory_space=pltpu.VMEM),) * 3,
            scratch_shapes=[
                vm((RANK, J_TILE), F32),
                vm((2 * K_LOC, RANK), F32),
                vm((J_TILES, K_LOC, I_LOC, J_TILE), F32),
                vm((J_TILES, K_LOC, I_LOC, J_TILE), BF16),
                vm((J_TILES, K_LOC, J_TILE, I_LOC), BF16),
                vm((K_LOC, RANK, I_LOC), F32),
                vm((SWEEPS + 1, J_TILES, RANK, J_TILE), BF16),
                vm((RANK, LANES), F32),
                vm((RANK, LANES), F32),
                vm((K_LOC, RANK, LANES), F32),
                vm((A_CHUNKS, RANK, I_HALF), F32),
                vm((A_CHUNKS, RANK, I_HALF), BF16),
                vm((A_CHUNKS, RANK, I_HALF), F32),
                vm((SWEEPS, 3, A_CHUNKS, RANK, I_HALF), F32),
                vm((RANK, LANES), F32),
                vm((SWEEPS, RANK, LANES), F32),
                vm((J_TILES, RANK, J_TILE), F32),
                vm((SWEEPS, 2, RANK, J_TILE), F32),
                vm((2, RANK, J_TILE), F32),
                vm((SWEEPS, 2, RANK, J_TILE), F32),
                vm((2, RANK, J_TILE), F32),
                vm((RANK // 2, LANES), F32),
                vm((7, RANK // 2, LANES), F32),
                vm((RANK // 2, LANES), F32),
                vm((SWEEPS, 3, RANK // 2, LANES), F32),
                vm((RANK, LANES), F32),
                vm((K_LOC // 2, LANES), F32),
                vm((SWEEPS, 7, K_LOC // 2, LANES), F32),
                vm((RANK, RANK), F32),
                dma((2,)), dma((J_TILES, K_LOC // LOAD_K)), dma((3,)), dma((3,)),
                dma((3, A_CHUNKS)), dma((SWEEPS, 3, A_CHUNKS)),
                dma, dma((SWEEPS,)),
                dma((2,)), dma((SWEEPS, 2)), dma((2,)), dma((SWEEPS, 2)),
                dma((2,)), dma((SWEEPS, 2)),
                dma((7,)), dma((7,)), dma((3,)), dma((SWEEPS, 3)),
                dma((7,)), dma((SWEEPS, 7)),
            ],
            compiler_params=pltpu.CompilerParams(collective_id=0, has_side_effects=True,
                                                 vmem_limit_bytes=52 * 1024 * 1024),
            name="als_sweeps",
        )(*operands, ridge_lam.reshape(1, 1))
        a_new, b_new, c_new = pl.pallas_call(
            emit,
            out_shape=tuple(jax.ShapeDtypeStruct(shape, F32) for shape in shapes),
            in_specs=[pl.BlockSpec(memory_space=pltpu.VMEM)] * 3,
            out_specs=(pl.BlockSpec(memory_space=pl.ANY),) * 3,
            scratch_shapes=[dma((3,))],
            compiler_params=pltpu.CompilerParams(vmem_limit_bytes=1024 * 1024),
            name="emit_factors",
        )(a_new, b_new, c_new)
        return a_new, b_new.T, c_new

    return jax.shard_map(
        local,
        mesh=mesh,
        in_specs=(P("tube", "row", "col"), P(("col", "row", "tube"), None), P(None, None), P()),
        out_specs=(P(("row", "col", "tube"), None), P(("col", "row", "tube"), None), P(None, None)),
        check_vma=False,
    )
```

time: 46.2 us -> 45 us (0.974)
  Pallas kernels: 44.7 us -> 43.6 us
    pallas_call x1, Pallas kernels: 44 us -> 43 us  [local(): pl.pallas_call(kernel, out_shape=tuple((pltpu.VMEM(shape, F32) for shape...]
where the time goes in v4:
time: 45 us; the launch traced here: 44.9 us
  Pallas kernels  43.6 us (97%)
  between operations  1.29 us (3%)
    pallas_call x1, Pallas kernels, local(): pl.pallas_call(kernel, out_shape=tuple((pltpu.VMEM(shape, F32) for shape...  43 us

profile of v4, /device:TPU:0, one launch (start us, length us, event | category | flops | bytes accessed | tf_op | source)
XLA Modules:
  0.0 44.9 jit_solution(10108375208082346773)
XLA Ops:
  1.3 43.0 %als_sweeps.1 = (f32[64,64]{1,0:T(8,128)S(1)}, f32[64,256]{1,0:T(8,128)S(1)}, f32[32,64]{1,0:T(8,128)S(1)}) custom-call(f32[16,256,1024]{2,1,0:T(8,128)} %x_hbm.1, f32[64,256]{1,0:T(8,128)} %bitcast.4, f32[32,64]{1,0:T(8,128)} %c_hbm.1, f32[1,1]{1,0:T(1,128)} %bitcast.3.lam_ref), custom_call_target="tpu_custom_call" | custom-call | tf_op jit(solution)/shard_map/als_sweeps/pallas_call | solution.py:434
  44.2 0.7 %emit_factors.1 = (f32[64,64]{1,0:T(8,128)}, f32[64,256]{1,0:T(8,128)}, f32[32,64]{1,0:T(8,128)}) custom-call(f32[64,64]{1,0:T(8,128)S(1)} %get-tuple-element.9.a_in, f32[64,256]{1,0:T(8,128)S(1)} %get-tuple-element.10.b_in, f32[32,64]{1,0:T(8,128)S(1)} %get-tuple-element.11.c_in), custom_call_target="tpu_custom_call" | custom-call | tf_op jit(solution)/shard_map/emit_factors/pallas_call | solution.py:481

commit v5 on v4

--- a/solution.py
+++ b/solution.py
@@ -87,7 +87,7 @@
 def kernel(x_hbm, b_hbm, c_hbm, lam_ref, a_out, b_out, c_out,
            b_init, c_init, xf, x4, x4t, u_ref, bt, c_own, c_other, cb, a32_ref, at_ref,
            ma_snd, ma_rcv, ga_snd, ga_rcv, mb_part, mb_d2d, mb_sum, mb_rcv, bo_ref,
-           g0_snd, g0_rcv, gb_snd, gb_rcv, gb_all, mc_snd, mc_rcv, inv_ref,
+           g0_snd, g0_rcv, gb_part, gb_snd, gb_rcv, gb_all, mc_snd, mc_rcv, inv_ref,
            in_sem, x_sem, b_ss, b_rs, ma_ss, ma_rs, ga_ss, ga_rs, md_ss, md_rs, my_ss, my_rs,
            ag_ss, ag_rs, g0_ss, g0_rs, gb_ss, gb_rs, mc_ss, mc_rs):
     tube, col, row = lax.axis_index("tube"), lax.axis_index("col"), lax.axis_index("row")
@@ -186,9 +186,13 @@
         return send(gb_snd, gb_rcv.at[s, d - 1], gb_ss.at[d - 1], gb_rs.at[s, d - 1], d)
 
     def gram_b_start(s):
-        gb_snd[...] = gram_pack([bt[s + 1, row * 2], bt[s + 1, row * 2 + 1]])
-        for d in (2, 3, 1):
-            gb_send(s, d).start()
+        gb_snd[...] = gb_part[...] + gram_pack([bt[s + 1, row * 2 + 1]])
+        for core in range(2):
+            n = 1 + (row if core == 0 else 1 - row)
+            pltpu.make_async_remote_copy(src_ref=gb_snd, dst_ref=gb_rcv.at[s, n], send_sem=gb_ss.at[n],
+                                         recv_sem=gb_rs.at[s, n], device_id=(tube, 1 - col, core),
+                                         device_id_type=MESH).start()
+        gb_send(s, 1).start()
 
     def gram_b_finish(s):
         for d in (3, 2, 1):
@@ -257,11 +261,15 @@
         for d in range(1, 8):
             c_send(s, d).wait_send()
 
+    def c_near(s):
+        c_own[...] = c_solve((mc_snd[...] + mc_rcv[s, 0]) + (mc_rcv[s, 1] + mc_rcv[s, 2]))
+
     def c_far(s):
+        c_other[...] = c_solve((mc_rcv[s, 3] + mc_rcv[s, 4]) + (mc_rcv[s, 5] + mc_rcv[s, 6]))
+
+    def c_far_wait(s):
         for d in (4, 5, 6, 7):
             c_send(s, d).wait_recv()
-        far = (mc_rcv[s, 3] + mc_rcv[s, 4]) + (mc_rcv[s, 5] + mc_rcv[s, 6])
-        c_other[...] = c_solve(far)
 
     @pl.loop(0, SWEEPS)
     def _(s):
@@ -279,6 +287,7 @@
 
         @pl.when(s > 0)
         def _():
+            c_far_wait(s - 1)
             c_far(s - 1)
 
         gram_c = gram_dup(c_own[...].astype(BF16)) + gram_dup(c_other[...].astype(BF16))
@@ -374,12 +383,14 @@
             g_copies.append(cp)
 
         b_solve(0)
+        gb_part[...] = gram_pack([bt[s + 1, row * 2]])
         b_solve(1)
         gram_b_start(s)
         u_pass(s + 1, [row * 2, row * 2 + 1], True, False)
-        for cp in g_copies:
-            cp.wait_recv()
-        part_c = u_pass(s + 1, [(1 - row) * 2, (1 - row) * 2 + 1], False, True)
+        g_copies[0].wait_recv()
+        u_pass(s + 1, [(1 - row) * 2], False, False)
+        g_copies[1].wait_recv()
+        part_c = u_pass(s + 1, [(1 - row) * 2 + 1], False, True)
 
         @pl.when(s > 0)
         def _():
@@ -388,6 +399,9 @@
         mc_snd[...] = part_c
         for d in (6, 7, 2, 3, 4, 5, 1):
             c_send(s, d).start()
+        a_rows = a32_ref[col].T
+        a_out[...] = jnp.where(tube == 0, a_rows[:I_HALF // 2], a_rows[I_HALF // 2:])
+        b_out[...] = bo_ref[tube]
         gram_b_finish(s)
         inv_ref[...] = spd_inverse(gram_a * gb_all[...], lam)
         for ch in range(A_CHUNKS):
@@ -402,15 +416,16 @@
             gb_send(s, d).wait_send()
         for d in (1, 2, 3):
             c_send(s, d).wait_recv()
-        near = (mc_snd[...] + mc_rcv[s, 0]) + (mc_rcv[s, 1] + mc_rcv[s, 2])
-        c_own[...] = c_solve(near)
-        spread_c()
-
+
+        @pl.when(s < SWEEPS - 1)
+        def _():
+            c_near(s)
+            spread_c()
+
+    c_far_wait(SWEEPS - 1)
+    c_near(SWEEPS - 1)
     c_far(SWEEPS - 1)
     c_sent(SWEEPS - 1)
-    a_rows = a32_ref[col].T
-    a_out[...] = jnp.where(tube == 0, a_rows[:I_HALF // 2], a_rows[I_HALF // 2:])
-    b_out[...] = bo_ref[tube]
     c_out[pl.ds(k_base, K_LOC), :] = c_own[...].T[:K_LOC]
     c_out[pl.ds(k_far, K_LOC), :] = c_other[...].T[:K_LOC]
 
@@ -461,6 +476,7 @@
                 vm((RANK // 2, LANES), F32),
                 vm((7, RANK // 2, LANES), F32),
                 vm((RANK // 2, LANES), F32),
+                vm((RANK // 2, LANES), F32),
                 vm((SWEEPS, 3, RANK // 2, LANES), F32),
                 vm((RANK, LANES), F32),
                 vm((K_LOC // 2, LANES), F32),

time: 45 us -> 44 us (0.978)
  Pallas kernels: 43.6 us -> 42.7 us
    pallas_call x1, Pallas kernels: 43 us -> 42 us  [local(): pl.pallas_call(kernel, out_shape=tuple((pltpu.VMEM(shape, F32) for shape...]
where the time goes in v5:
time: 44 us; the launch traced here: 43.9 us
  Pallas kernels  42.7 us (97%)
  between operations  1.29 us (3%)
    pallas_call x1, Pallas kernels, local(): pl.pallas_call(kernel, out_shape=tuple((pltpu.VMEM(shape, F32) for shape...  42 us

profile of v5, /device:TPU:0, one launch (start us, length us, event | category | flops | bytes accessed | tf_op | source)
XLA Modules:
  0.0 43.9 jit_solution(1929299897500350822)
XLA Ops:
  1.3 42.0 %als_sweeps.1 = (f32[64,64]{1,0:T(8,128)S(1)}, f32[64,256]{1,0:T(8,128)S(1)}, f32[32,64]{1,0:T(8,128)S(1)}) custom-call(f32[16,256,1024]{2,1,0:T(8,128)} %x_hbm.1, f32[64,256]{1,0:T(8,128)} %bitcast.4, f32[32,64]{1,0:T(8,128)} %c_hbm.1, f32[1,1]{1,0:T(1,128)} %bitcast.3.lam_ref), custom_call_target="tpu_custom_call" | custom-call | tf_op jit(solution)/shard_map/als_sweeps/pallas_call | solution.py:449
  43.3 0.7 %emit_factors.1 = (f32[64,64]{1,0:T(8,128)}, f32[64,256]{1,0:T(8,128)}, f32[32,64]{1,0:T(8,128)}) custom-call(f32[64,64]{1,0:T(8,128)S(1)} %get-tuple-element.9.a_in, f32[64,256]{1,0:T(8,128)S(1)} %get-tuple-element.10.b_in, f32[32,64]{1,0:T(8,128)S(1)} %get-tuple-element.11.c_in), custom_call_target="tpu_custom_call" | custom-call | tf_op jit(solution)/shard_map/emit_factors/pallas_call | solution.py:497

commit v6 on v5

--- a/solution.py
+++ b/solution.py
@@ -1,5 +1,3 @@
-import functools
-
 import jax
 import jax.numpy as jnp
 from jax import lax
@@ -17,6 +15,7 @@
 I_HALF = I_LOC // 2
 A_CHUNKS = 2
 BLK = 16
+SUB = 8
 LOAD_K = 4
 MESH = pl.DeviceIdType.MESH
 HIGH = lax.Precision.HIGHEST
@@ -42,42 +41,51 @@
     left_eye = jnp.where(lane_ids == row_ids, 1.0, 0.0).astype(F32)
     right_eye = jnp.where(lane_ids == row_ids + RANK, 1.0, 0.0).astype(F32)
     aug = jnp.where(lane_ids < RANK, left_eye, gram_dup + lam * right_eye)
-    n_blk = RANK // BLK
-    blocks = [aug[b * BLK:(b + 1) * BLK] for b in range(n_blk)]
-    sub_ids = lax.broadcasted_iota(jnp.int32, (BLK, LANES), 0)
-
-    def lane(block, b, c):
-        at = RANK + b * BLK + c
-        return jnp.broadcast_to(block[:, at:at + 1], (BLK, LANES))
-
-    def sublane(block, c):
-        return jnp.broadcast_to(block[c:c + 1, :], (BLK, LANES))
+    groups = [aug[n * SUB:(n + 1) * SUB] for n in range(RANK // SUB)]
+    sub_ids = lax.broadcasted_iota(jnp.int32, (SUB, LANES), 0)
+    per_blk = BLK // SUB
+
+    def lane(group, at):
+        return jnp.broadcast_to(group[:, at:at + 1], (SUB, LANES))
+
+    def sublane(parts, c):
+        part = parts[c // SUB]
+        return jnp.broadcast_to(part[c % SUB:c % SUB + 1, :], (SUB, LANES))
 
     done = []
-    for b in range(n_blk):
-        piv = blocks[b]
-        cols = [lane(piv, b, c) for c in range(BLK)]
-        mults = [[lane(blocks[t], b, c) for c in range(BLK)] for t in range(b + 1, n_blk)]
-        chol_rows = jnp.zeros((BLK, LANES), F32)
+    for b in range(RANK // BLK):
+        first, start = b * per_blk, RANK + b * BLK
+        piv = groups[first:first + per_blk]
+        cols = [[lane(part, start + c) for part in piv] for c in range(BLK)]
+        rest = range(first + per_blk, RANK // SUB)
+        mults = {n: [lane(groups[n], start + c) for c in range(BLK)] for n in rest}
+        chol_rows = [jnp.zeros((SUB, LANES), F32) for _ in range(per_blk)]
         diag = sublane(cols[0], 0)
         for c in range(BLK):
-            is_row = sub_ids == c
+            is_row = sub_ids == c % SUB
+            home = c // SUB
             root = lax.rsqrt(diag)
             elts = {c2: sublane(cols[c2], c) * root for c2 in range(c + 1, BLK)}
             if c + 1 < BLK:
                 diag = sublane(cols[c + 1], c + 1) - (sublane(cols[c], c + 1) * root) * elts[c + 1]
-            scaled_col = cols[c] * root
+            scaled_col = [part * root for part in cols[c]]
             scaled_row = sublane(piv, c) * root
-            chol_rows = jnp.where(is_row, scaled_row, chol_rows)
-            piv = jnp.where(is_row, scaled_row * root, piv - scaled_col * scaled_row)
+
+            def eliminate(parts, elt):
+                new = [part - scale * elt for part, scale in zip(parts, scaled_col)]
+                new[home] = jnp.where(is_row, elt * root, new[home])
+                return new
+
+            chol_rows[home] = jnp.where(is_row, scaled_row, chol_rows[home])
+            piv = eliminate(piv, scaled_row)
             for c2 in range(c + 1, BLK):
-                cols[c2] = jnp.where(is_row, elts[c2] * root, cols[c2] - scaled_col * elts[c2])
-        done.append(chol_rows)
-        for t in range(b + 1, n_blk):
-            upd = blocks[t]
+                cols[c2] = eliminate(cols[c2], elts[c2])
+        done += chol_rows
+        for n in rest:
+            upd = groups[n]
             for c in range(BLK):
-                upd = upd - mults[t - b - 1][c] * sublane(piv, c)
-            blocks[t] = upd
+                upd = upd - mults[n][c] * sublane(piv, c)
+            groups[n] = upd
         if between is not None:
             between(b)
     low_inv = jnp.concatenate(done, axis=0)[:, :RANK]
@@ -185,7 +193,12 @@
     def gb_send(s, d):
         return send(gb_snd, gb_rcv.at[s, d - 1], gb_ss.at[d - 1], gb_rs.at[s, d - 1], d)
 
+    def gram_b_sent(s):
+        for d in (1, 2, 3):
+            gb_send(s, d).wait_send()
+
     def gram_b_start(s):
+        pl.when(s > 0)(lambda: gram_b_sent(s - 1))
         gb_snd[...] = gb_part[...] + gram_pack([bt[s + 1, row * 2 + 1]])
         for core in range(2):
             n = 1 + (row if core == 0 else 1 - row)
@@ -271,20 +284,29 @@
         for d in (4, 5, 6, 7):
             c_send(s, d).wait_recv()
 
+    def a_send(s, ch, d):
+        n = d // 2 - 1
+        return send(ma_snd.at[ch], ma_rcv.at[s, n, ch], ma_ss.at[n, ch], ma_rs.at[s, n, ch], d)
+
+    def a_start(s, spread):
+        parts = [jnp.zeros((RANK, I_HALF), F32) for _ in range(A_CHUNKS)]
+        for k in range(K_LOC):
+            if spread:
+                c_col = jnp.broadcast_to(c_own[:, k:k + 1], (RANK, LANES))
+                cb[k] = c_col
+            else:
+                c_col = cb[k]
+            for ch in range(A_CHUNKS):
+                parts[ch] = parts[ch] + u_ref[k, :, ch * I_HALF:(ch + 1) * I_HALF] * c_col
+        for ch in range(A_CHUNKS):
+            ma_snd[ch] = parts[ch]
+            for d in (6, 4, 2):
+                a_send(s, ch, d).start()
+
+    a_start(0, False)
+
     @pl.loop(0, SWEEPS)
     def _(s):
-        def a_send(ch, d):
-            n = d // 2 - 1
-            return send(ma_snd.at[ch], ma_rcv.at[s, n, ch], ma_ss.at[n, ch], ma_rs.at[s, n, ch], d)
-
-        for ch in range(A_CHUNKS):
-            part = jnp.zeros((RANK, I_HALF), F32)
-            for k in range(K_LOC):
-                part = part + u_ref[k, :, ch * I_HALF:(ch + 1) * I_HALF] * cb[k]
-            ma_snd[ch] = part
-            for d in (6, 4, 2):
-                a_send(ch, d).start()
-
         @pl.when(s > 0)
         def _():
             c_far_wait(s - 1)
@@ -294,7 +316,7 @@
         inv_a = spd_inverse(gb_all[...] * gram_c, lam)
         def a_solve(ch):
             for d in (2, 4, 6):
-                a_send(ch, d).wait_recv()
+                a_send(s, ch, d).wait_recv()
             mtt_a = (ma_snd[ch] + ma_rcv[s, 0, ch]) + (ma_rcv[s, 1, ch] + ma_rcv[s, 2, ch])
             a_turn = dot_nn(inv_a, mtt_a, HIGH)
             a32_ref[ch] = a_turn
@@ -399,33 +421,32 @@
         mc_snd[...] = part_c
         for d in (6, 7, 2, 3, 4, 5, 1):
             c_send(s, d).start()
+        for ch in range(A_CHUNKS):
+            for d in (2, 4, 6):
+                a_send(s, ch, d).wait_send()
+        ga_send().wait_send()
+        for q in range(2):
+            d_send(q).wait_send()
+            y_send(q).wait_send()
+            g_copies[q].wait_send()
         a_rows = a32_ref[col].T
         a_out[...] = jnp.where(tube == 0, a_rows[:I_HALF // 2], a_rows[I_HALF // 2:])
         b_out[...] = bo_ref[tube]
         gram_b_finish(s)
         inv_ref[...] = spd_inverse(gram_a * gb_all[...], lam)
-        for ch in range(A_CHUNKS):
-            for d in (2, 4, 6):
-                a_send(ch, d).wait_send()
-        ga_send().wait_send()
-        for q in range(2):
-            d_send(q).wait_send()
-            y_send(q).wait_send()
-            g_copies[q].wait_send()
-        for d in (1, 2, 3):
-            gb_send(s, d).wait_send()
         for d in (1, 2, 3):
             c_send(s, d).wait_recv()
 
         @pl.when(s < SWEEPS - 1)
         def _():
             c_near(s)
-            spread_c()
+            a_start(s + 1, True)
 
     c_far_wait(SWEEPS - 1)
     c_near(SWEEPS - 1)
     c_far(SWEEPS - 1)
     c_sent(SWEEPS - 1)
+    gram_b_sent(SWEEPS - 1)
     c_out[pl.ds(k_base, K_LOC), :] = c_own[...].T[:K_LOC]
     c_out[pl.ds(k_far, K_LOC), :] = c_other[...].T[:K_LOC]
 

time: 44 us -> 43.9 us (level)
  no operation moved by 1% of the time
where the time goes in v6:
time: 43.9 us; the launch traced here: 43.8 us
  Pallas kernels  42.5 us (97%)
  between operations  1.29 us (3%)
    pallas_call x1, Pallas kernels, local(): pl.pallas_call(kernel, out_shape=tuple((pltpu.VMEM(shape, F32) for shape...  41.8 us

profile of v6, /device:TPU:0, one launch (start us, length us, event | category | flops | bytes accessed | tf_op | source)
XLA Modules:
  0.0 43.8 jit_solution(9354149818047133387)
XLA Ops:
  1.3 41.8 %als_sweeps.1 = (f32[64,64]{1,0:T(8,128)S(1)}, f32[64,256]{1,0:T(8,128)S(1)}, f32[32,64]{1,0:T(8,128)S(1)}) custom-call(f32[16,256,1024]{2,1,0:T(8,128)} %x_hbm.1, f32[64,256]{1,0:T(8,128)} %bitcast.4, f32[32,64]{1,0:T(8,128)} %c_hbm.1, f32[1,1]{1,0:T(1,128)} %bitcast.3.lam_ref), custom_call_target="tpu_custom_call" | custom-call | tf_op jit(solution)/shard_map/als_sweeps/pallas_call | solution.py:470
  43.1 0.7 %emit_factors.1 = (f32[64,64]{1,0:T(8,128)}, f32[64,256]{1,0:T(8,128)}, f32[32,64]{1,0:T(8,128)}) custom-call(f32[64,64]{1,0:T(8,128)S(1)} %get-tuple-element.9.a_in, f32[64,256]{1,0:T(8,128)S(1)} %get-tuple-element.10.b_in, f32[32,64]{1,0:T(8,128)S(1)} %get-tuple-element.11.c_in), custom_call_target="tpu_custom_call" | custom-call | tf_op jit(solution)/shard_map/emit_factors/pallas_call | solution.py:518

commit v7 on v6

--- a/solution.py
+++ b/solution.py
@@ -371,13 +371,20 @@
 
         ga_send().start()
         v_last(1)
+
+        @pl.when(row == 0)
+        def _():
+            reduce_cores(1)
+
+        @pl.when(row == 1)
+        def _():
+            d_send(1).start()
+
         v_last(3)
 
         @pl.when(row == 0)
         def _():
-            reduce_cores(1)
-
-        d_send(1).start()
+            d_send(1).start()
 
         def late_reduce(b):
             if b == 0:

time: 43.9 us -> 43.6 us (level)
  no operation moved by 1% of the time
where the time goes in v7:
time: 43.6 us; the launch traced here: 43.5 us
  Pallas kernels  42.2 us (97%)
  between operations  1.29 us (3%)
    pallas_call x1, Pallas kernels, local(): pl.pallas_call(kernel, out_shape=tuple((pltpu.VMEM(shape, F32) for shape...  41.5 us

profile of v7, /device:TPU:0, one launch (start us, length us, event | category | flops | bytes accessed | tf_op | source)
XLA Modules:
  0.0 43.5 jit_solution(187498580697685647)
XLA Ops:
  1.3 41.5 %als_sweeps.1 = (f32[64,64]{1,0:T(8,128)S(1)}, f32[64,256]{1,0:T(8,128)S(1)}, f32[32,64]{1,0:T(8,128)S(1)}) custom-call(f32[16,256,1024]{2,1,0:T(8,128)} %x_hbm.1, f32[64,256]{1,0:T(8,128)} %bitcast.4, f32[32,64]{1,0:T(8,128)} %c_hbm.1, f32[1,1]{1,0:T(1,128)} %bitcast.3.lam_ref), custom_call_target="tpu_custom_call" | custom-call | tf_op jit(solution)/shard_map/als_sweeps/pallas_call | solution.py:477
  42.8 0.7 %emit_factors.1 = (f32[64,64]{1,0:T(8,128)}, f32[64,256]{1,0:T(8,128)}, f32[32,64]{1,0:T(8,128)}) custom-call(f32[64,64]{1,0:T(8,128)S(1)} %get-tuple-element.9.a_in, f32[64,256]{1,0:T(8,128)S(1)} %get-tuple-element.10.b_in, f32[32,64]{1,0:T(8,128)S(1)} %get-tuple-element.11.c_in), custom_call_target="tpu_custom_call" | custom-call | tf_op jit(solution)/shard_map/emit_factors/pallas_call | solution.py:525

commit v8 on v7

--- a/solution.py
+++ b/solution.py
@@ -362,23 +362,23 @@
         def _():
             d_send(0).start()
 
+        v_last(1)
+        ga_snd[...] = sum(gram_dup(at_ref[ch]) for ch in range(A_CHUNKS))
+
+        @pl.when(row == 0)
+        def _():
+            reduce_cores(1)
+
+        @pl.when(row == 1)
+        def _():
+            d_send(1).start()
+
+        ga_send().start()
         v_last(2)
-        ga_snd[...] = sum(gram_dup(at_ref[ch]) for ch in range(A_CHUNKS))
 
         @pl.when(row == 0)
         def _():
             d_send(0).start()
-
-        ga_send().start()
-        v_last(1)
-
-        @pl.when(row == 0)
-        def _():
-            reduce_cores(1)
-
-        @pl.when(row == 1)
-        def _():
-            d_send(1).start()
 
         v_last(3)
 

time: 43.6 us -> 43.5 us (level)
  no operation moved by 1% of the time
where the time goes in v8:
time: 43.5 us; the launch traced here: 43.4 us
  Pallas kernels  42.2 us (97%)
  between operations  1.29 us (3%)
    pallas_call x1, Pallas kernels, local(): pl.pallas_call(kernel, out_shape=tuple((pltpu.VMEM(shape, F32) for shape...  41.5 us

profile of v8, /device:TPU:0, one launch (start us, length us, event | category | flops | bytes accessed | tf_op | source)
XLA Modules:
  0.0 43.4 jit_solution(17117753938151458361)
XLA Ops:
  1.3 41.5 %als_sweeps.1 = (f32[64,64]{1,0:T(8,128)S(1)}, f32[64,256]{1,0:T(8,128)S(1)}, f32[32,64]{1,0:T(8,128)S(1)}) custom-call(f32[16,256,1024]{2,1,0:T(8,128)} %x_hbm.1, f32[64,256]{1,0:T(8,128)} %bitcast.4, f32[32,64]{1,0:T(8,128)} %c_hbm.1, f32[1,1]{1,0:T(1,128)} %bitcast.3.lam_ref), custom_call_target="tpu_custom_call" | custom-call | tf_op jit(solution)/shard_map/als_sweeps/pallas_call | solution.py:477
  42.8 0.7 %emit_factors.1 = (f32[64,64]{1,0:T(8,128)}, f32[64,256]{1,0:T(8,128)}, f32[32,64]{1,0:T(8,128)}) custom-call(f32[64,64]{1,0:T(8,128)S(1)} %get-tuple-element.9.a_in, f32[64,256]{1,0:T(8,128)S(1)} %get-tuple-element.10.b_in, f32[32,64]{1,0:T(8,128)S(1)} %get-tuple-element.11.c_in), custom_call_target="tpu_custom_call" | custom-call | tf_op jit(solution)/shard_map/emit_factors/pallas_call | solution.py:525
